TPU v7x, 32 devices: a whole 2x2x4 slice. The times are simulated.
32 devices in a mesh: groups: 2 (over y), gx: 16 (over z, x, core).
Axes of the slice: x: 2, y: 2, z: 4, core: 2. Of those that a mesh axis runs over, the one named last changes fastest.
Arguments:
- stream_in: bfloat16 [32, 8192], P(('groups', 'gx')), parts along dimension 0, may hold values from -6 to 6
- query: bfloat16 [32, 8192], P(('groups', 'gx')), parts along dimension 0, may hold values from -4.5 to 4.5
- key_new: bfloat16 [32, 1024], P(('groups', 'gx')), parts along dimension 0, may hold values from -4.5 to 4.5
- value_new: bfloat16 [32, 1024], P(('groups', 'gx')), parts along dimension 0, may hold values from -6 to 6
- key_cache: bfloat16 [32, 128, 1024], P(('groups', 'gx')), parts along dimension 0, may hold values from -6 to 6
- value_cache: bfloat16 [32, 128, 1024], P(('groups', 'gx')), parts along dimension 0, may hold values from -6 to 6
- lengths: int32 [32], P(('groups', 'gx')), parts along dimension 0, may hold values from 1 to 128, as said below
- route_ids: int32 [32, 2], P(('groups', 'gx')), parts along dimension 0, may hold values from 0 to 3, as said below
- route_scores: float32 [32, 2], P(('groups', 'gx')), parts along dimension 0, may hold values from -6 to 6
- out_weight: bfloat16 [8192, 8192], P(None, 'gx'), may hold values from -0.0625 to 0.0625
- norm_gain: float32 [8192], replicated, may hold values from 0.1 to 1.9
- gate_weight: bfloat16 [2, 16384, 7168], P(None, 'gx'), may hold values from -0.0625 to 0.0625
- up_weight: bfloat16 [2, 16384, 7168], P(None, 'gx'), may hold values from -0.0625 to 0.0625
- down_weight: bfloat16 [2, 114688, 1024], P(None, 'gx'), may hold values from -0.046875 to 0.046875
Outputs:
- layer_out: bfloat16 [32, 8192], P(('groups', 'gx')), parts along dimension 0
There are 2 independent parts, one for each index of `groups`. A program takes and returns all parts, laid end to end along the dimension named above; an argument that names none is the same for every part. Nothing has to cross between parts.
Inputs may be any that keep to these rules, and one draw needn't show every extreme that they name: `lengths`: 1 to 128; some sequence fills all 128 slots. `route_ids`: each row names two different experts of 0 to 3; in one replica's batch each of the experts 0 and 1 is named by at most 10 sequences, and one of them by exactly 10.
All inputs are finite; a program needn't handle non-finite values.
Results may differ from a plain program's by a relative error of at most 0.0095.
Values may be sent and summed in bfloat16 or wider, within the bound.
A program may use at most 192 MiB of HBM per device.

v0:
```python
import functools

import jax
import jax.numpy as jnp
from jax import lax
from jax.experimental import pallas as pl
from jax.experimental.pallas import tpu as pltpu
from jax.sharding import PartitionSpec as P

NH = 64
KVH = 8
HS = 128
RESIDENT = 2
MSPLIT = 8
PAD = 16
RING = 3
ORDER = (0, 2, 1, 3)
MESH = pl.DeviceIdType.MESH


def kernel(
    members,
    query,
    key_new,
    value_new,
    key_hbm,
    value_hbm,
    lengths,
    route_ids,
    route_scores,
    stream,
    gain,
    out_weight,
    gate_weight,
    up_weight,
    down_weight,
    out,
    key_cache,
    value_cache,
    cache_sem,
    heads,
    own_rows,
    stream_rows,
    wo,
    gu,
    down,
    attn_send,
    attn_recv,
    attn_wide,
    attn_rows,
    stream_recv,
    resid_recv,
    resid_send,
    sq_send,
    sq_recv,
    normed,
    slots_in,
    acc,
    part_send,
    part_recv,
    hid_send,
    hid_recv,
    total,
    resid_full,
    final_send,
    final_recv,
    wo_sem,
    gu_sem,
    down_sem,
    a_send,
    a_relay,
    a_recv,
    s_send,
    s_recv,
    q_send,
    q_recv,
    r_send,
    r_recv,
    p_send,
    p_recv,
    h_send,
    h_relay,
    h_recv,
    f_send,
    f_recv,
):
    f32, bf16 = jnp.float32, jnp.bfloat16
    hsplit = members // MSPLIT
    me = lax.axis_index("gx")
    m = me // hsplit
    h = lax.rem(me, hsplit)
    batch = members
    cols = wo.shape[1]
    width = cols * members
    block = width // MSPLIT
    group = NH // KVH
    chunk = gu.shape[3]
    chunks = gate_weight.shape[2] // chunk
    narrow = part_send.shape[2]
    cap = batch * 5 // 8
    packed = part_send.shape[1]
    hid_rows = hid_send.shape[0]
    lead = slots_in.shape[1]
    lanes = sq_send.shape[1]
    ring = gu.shape[0]

    def peer(d):
        return lax.rem(me + d, members)

    def model(d):
        d = jnp.asarray(d, jnp.int32)
        to = 0
        for b in (1, 2, 4):
            to = to + lax.rem(lax.div(m, b) + lax.div(d, b), 2) * b
        return to

    def mate(d):
        return lax.rem(h + d, hsplit)

    def remote(src, dst, send, recv, device):
        return pltpu.make_async_remote_copy(
            src_ref=src,
            dst_ref=dst,
            send_sem=send,
            recv_sem=recv,
            device_id={"gx": device},
            device_id_type=MESH,
        )

    barrier = pltpu.get_barrier_semaphore()

    @pl.loop(1, members)
    def _(d):
        pl.semaphore_signal(barrier, inc=1, device_id={"gx": peer(d)}, device_id_type=MESH)

    key_copy = pltpu.make_async_copy(key_hbm, key_cache, cache_sem.at[0])
    value_copy = pltpu.make_async_copy(value_hbm, value_cache, cache_sem.at[1])
    key_copy.start()
    value_copy.start()
    wo_copy = pltpu.make_async_copy(out_weight, wo, wo_sem)
    wo_copy.start()

    def gu_copy(i, q):
        r, w = q // 2, (gate_weight, up_weight)[q % 2]
        if chunks == 1:
            src = w.at[r]
        else:
            at = pl.multiple_of(model(MSPLIT - 1 - i) * chunk, 128)
            src = w.at[r, :, pl.ds(at, chunk)]
        slot = lax.rem(i, ring)
        return pltpu.make_async_copy(src, gu.at[slot, q], gu_sem.at[slot, q])

    def down_copy(i, r):
        at = pl.multiple_of(model(i) * narrow, 16)
        return pltpu.make_async_copy(
            down_weight.at[r, pl.ds(at, narrow), :], down.at[i, r], down_sem.at[i, r]
        )

    @pl.loop(0, ring)
    def _(i):
        for q in range(4):
            gu_copy(i, q).start()

    @pl.loop(0, MSPLIT)
    def _(i):
        for r in range(RESIDENT):
            down_copy(i, r).start()

    scale = HS ** (-0.5)
    for n in range(NH):
        heads[n : n + 1, :] = query[:, n * HS : (n + 1) * HS].astype(f32)
    for g in range(KVH):
        own_rows[0, g : g + 1, :] = key_new[:, g * HS : (g + 1) * HS].astype(f32)
        own_rows[1, g : g + 1, :] = value_new[:, g * HS : (g + 1) * HS].astype(f32)
    for j in range(members):
        stream_rows[j] = stream[:, j * cols : (j + 1) * cols].astype(f32)
    wide_q = heads[...]
    key_copy.wait()
    value_copy.wait()
    s = jnp.concatenate(
        [
            lax.dot_general(
                wide_q[g * group : (g + 1) * group].astype(bf16),
                key_cache[:, g * HS : (g + 1) * HS],
                (((1,), (1,)), ((), ())),
                preferred_element_type=f32,
            )
            for g in range(KVH)
        ],
        axis=0,
    )
    s = s * scale
    live = lax.broadcasted_iota(jnp.int32, s.shape, 1) < lengths[0]
    s = jnp.where(live, s, -1e30)
    k_own, v_own = own_rows[0], own_rows[1]
    spread = lambda v: jnp.concatenate(
        [jnp.broadcast_to(v[g : g + 1], (group, HS)) for g in range(KVH)], axis=0
    )
    own = jnp.sum(wide_q * spread(k_own), axis=-1, keepdims=True) * scale
    top = jnp.maximum(jnp.max(s, axis=-1, keepdims=True), own)
    e_cache = jnp.exp(s - top)
    e_own = jnp.exp(own - top)
    norm = jnp.sum(e_cache, axis=-1, keepdims=True) + e_own
    p = e_cache / norm
    p_own = (e_own / norm).astype(bf16).astype(f32)
    mixed = jnp.concatenate(
        [
            jnp.dot(
                p[g * group : (g + 1) * group].astype(bf16),
                value_cache[:, g * HS : (g + 1) * HS],
                preferred_element_type=f32,
            )
            for g in range(KVH)
        ],
        axis=0,
    )
    mixed = mixed + p_own * spread(v_own)
    attn_send[:NH, :] = mixed.astype(bf16)
    full = lambda v: jnp.full((PAD, HS), v)
    s0, s1 = full(route_scores[0, 0]), full(route_scores[0, 1])
    i0, i1 = full(route_ids[0, 0]), full(route_ids[0, 1])
    peak = jnp.maximum(s0, s1)
    x0, x1 = jnp.exp(s0 - peak), jnp.exp(s1 - peak)
    row = lax.broadcasted_iota(jnp.int32, (PAD, HS), 0)
    pick = jnp.where(i0 == row, x0 / (x0 + x1), 0.0) + jnp.where(i1 == row, x1 / (x0 + x1), 0.0)
    attn_send[NH:, :] = pick.astype(bf16)

    pl.semaphore_wait(barrier, members - 1)

    def attn_copy(d, slot):
        return remote(
            attn_send, attn_recv.at[slot], a_send.at[d], a_recv.at[slot], model(d) * hsplit + h
        )

    def attn_relay(d, t, slot):
        src = attn_send if isinstance(d, int) else attn_recv.at[slot]
        return remote(
            src, attn_recv.at[slot], a_relay.at[d, t], a_recv.at[slot], m * hsplit + t
        )

    def stream_copy(to, slot):
        return remote(
            stream_rows.at[to], stream_recv.at[slot], s_send.at[to], s_recv.at[slot], to
        )

    @pl.loop(0, MSPLIT - 1)
    def _(i):
        attn_copy(MSPLIT - 1 - i, me).start()

    @pl.loop(1, hsplit)
    def _(d):
        attn_relay(0, mate(d), me).start()

    @pl.loop(1, members)
    def _(d):
        stream_copy(peer(d), me).start()

    attn_recv[me] = attn_send[...]
    stream_recv[me] = stream_rows[me]

    @pl.loop(1, MSPLIT)
    def _(i):
        slot = model(i) * hsplit + h
        attn_copy(i, slot).wait_recv()

        @pl.loop(1, hsplit)
        def _(d):
            attn_relay(i, mate(d), slot).start()

    @pl.loop(0, MSPLIT)
    def _(i):
        @pl.loop(1, hsplit)
        def _(d):
            attn_copy(i, model(i) * hsplit + mate(d)).wait_recv()

    stride = NH + PAD

    @pl.loop(0, members)
    def _(j):
        attn_wide[pl.ds(j * stride, stride), :] = attn_recv[j].astype(f32)

    for n in range(NH):
        attn_rows[:, n * HS : (n + 1) * HS] = attn_wide[pl.ds(n, batch, stride=stride), :].astype(
            bf16
        )
    scales = [attn_wide[pl.ds(NH + r, batch, stride=stride), :][:, :1] for r in range(RESIDENT)]

    sub = lax.broadcasted_iota(jnp.int32, (batch, batch), 0)
    lane = lax.broadcasted_iota(jnp.int32, (batch, batch), 1)
    named, rank, back = [], [], []
    for r in range(RESIDENT):
        col = jnp.where(scales[r] > 0.0, 1.0, 0.0)
        row = jnp.sum(jnp.where(sub == lane, col, 0.0), axis=0, keepdims=True)
        named.append(row)
        rank.append(jnp.sum(jnp.where(sub < lane, col, 0.0), axis=0, keepdims=True))
        place = jnp.sum(jnp.where(lane < sub, row, 0.0), axis=1, keepdims=True)
        at = lax.broadcasted_iota(jnp.int32, (batch, hid_rows), 1)
        hit = at == place.astype(jnp.int32) + r * cap
        back.append(jnp.where(hit, scales[r], 0.0))

    wo_copy.wait()
    proj = jnp.dot(attn_rows[...], wo[...], preferred_element_type=f32).astype(bf16)

    @pl.loop(1, members)
    def _(d):
        stream_copy(me, peer(d)).wait_recv()

    @pl.loop(0, members)
    def _(j):
        resid_send[pl.ds(j, 1), :] = stream_recv[j]

    resid = resid_send[...] + proj.astype(f32)
    resid_send[...] = resid
    sub_w = lax.broadcasted_iota(jnp.int32, (batch, lanes), 0)
    lane_w = lax.broadcasted_iota(jnp.int32, (batch, lanes), 1)
    squares = jnp.sum(resid * resid, axis=-1, keepdims=True)
    sq_send[...] = jnp.sum(jnp.where(sub_w == lane_w, squares, 0.0), axis=0, keepdims=True)

    def sq_copy(to, slot):
        return remote(sq_send, sq_recv.at[slot], q_send.at[to], q_recv.at[slot], to)

    def resid_copy(to, slot):
        return remote(
            resid_send, resid_recv.at[slot], r_send.at[to], r_recv.at[slot], m * hsplit + to
        )

    @pl.loop(1, members)
    def _(d):
        sq_copy(peer(d), me).start()

    @pl.loop(1, hsplit)
    def _(d):
        resid_copy(mate(d), h).start()

    sq_recv[me] = sq_send[...]
    resid_recv[h] = resid_send[...]

    @pl.loop(1, hsplit)
    def _(d):
        resid_copy(h, mate(d)).wait_recv()

    @pl.loop(1, members)
    def _(d):
        sq_copy(me, peer(d)).wait_recv()

    squares = jnp.sum(sq_recv[...], axis=0)
    squares = jnp.sum(jnp.where(sub_w == lane_w, squares, 0.0), axis=1, keepdims=True)
    power = squares * (1.0 / width)
    inverse = lax.rsqrt(power + 1e-05)
    block_resid = jnp.concatenate([resid_recv[j] for j in range(hsplit)], axis=1)
    normed[...] = (block_resid * inverse * gain[m]).astype(bf16)

    bases = [q * cap // 8 * 8 for q in range(4)]
    for q in range(4):
        r = q % 2
        shift = q * cap - bases[q]
        at = lax.broadcasted_iota(jnp.int32, (lead, batch), 0)
        hit = (at == rank[r].astype(jnp.int32) + shift) & (named[r] > 0.0)
        slots_in[q] = jnp.dot(
            jnp.where(hit, 1.0, 0.0).astype(bf16), normed[...], preferred_element_type=f32
        ).astype(bf16)
    acc[...] = jnp.zeros_like(acc)

    def part_copy(to, slot):
        return remote(
            part_send.at[to],
            part_recv.at[slot],
            p_send.at[to],
            p_recv.at[slot],
            to * hsplit + h,
        )

    def gather(slot, q):
        return jnp.dot(
            slots_in[ORDER[q]], gu[slot, q], preferred_element_type=f32
        ), pl.ds(bases[ORDER[q]], lead)

    if chunks == 1:
        for q in range(4):
            gu_copy(0, q).wait()
            value, rows = gather(0, q)
            acc[rows, :] += value
        for to in range(MSPLIT):
            part_send[to] = acc[:packed, to * narrow : (to + 1) * narrow].astype(bf16)

        @pl.loop(1, MSPLIT)
        def _(d):
            part_copy(model(d), m).start()

    else:

        @pl.loop(0, MSPLIT)
        def _(i):
            slot = lax.rem(i, ring)
            to = model(MSPLIT - 1 - i)
            for q in range(4):
                gu_copy(i, q).wait()
                value, rows = gather(slot, q)
                acc[rows, :] += value

                @pl.when(i < MSPLIT - ring)
                def _():
                    gu_copy(i + ring, q).start()

            part_send[to] = acc[:packed, :].astype(bf16)
            acc[...] = jnp.zeros_like(acc)

            @pl.when(i < MSPLIT - 1)
            def _():
                part_copy(to, m).start()

    @pl.loop(1, MSPLIT)
    def _(d):
        part_copy(m, model(d)).wait_recv()

    part_recv[m] = part_send[m]
    acc[:packed, :narrow] = jnp.sum(part_recv[...].astype(f32), axis=0)
    a = acc[:hid_rows, :narrow]
    b = acc[2 * cap : 2 * cap + hid_rows, :narrow]
    hid_send[...] = (a / (1.0 + jnp.exp(-a)) * b).astype(bf16)

    def hid_copy(d, slot):
        return remote(
            hid_send, hid_recv.at[slot], h_send.at[d], h_recv.at[slot], model(d) * hsplit + h
        )

    def hid_relay(j, slot):
        return remote(
            hid_recv.at[slot],
            hid_recv.at[slot],
            h_relay.at[j],
            h_recv.at[slot],
            model(1) * hsplit + h,
        )

    hid_copy(1, m).start()

    @pl.loop(1, MSPLIT // 2)
    def _(j):
        hid_copy(MSPLIT - 2 * j, m).start()

    hid_recv[m] = hid_send[...]
    total[...] = jnp.zeros_like(total)

    def expert_sums(i, slot):
        for r in range(RESIDENT):
            down_copy(i, r).wait()
            total[r] += jnp.dot(hid_recv[slot], down[i, r], preferred_element_type=f32)

    @pl.loop(0, MSPLIT // 2)
    def _(j):
        even, odd = model(2 * j), model(2 * j + 1)

        @pl.when(j > 0)
        def _():
            hid_copy(2 * j, even).wait_recv()
            hid_relay(j, even).start()

        expert_sums(2 * j, even)
        hid_copy(1, odd).wait_recv()
        expert_sums(2 * j + 1, odd)

    whole = jnp.where(h == 0, 1.0, 0.0) * block_resid
    for r in range(RESIDENT):
        if batch > 32:
            whole = whole + jnp.dot(
                back[r], total[r], precision=lax.Precision.HIGHEST, preferred_element_type=f32
            )
        else:
            for n in range(r * cap, (r + 1) * cap):
                whole = whole + back[r][:, n : n + 1] * total[r, n : n + 1, :]
    resid_full[...] = whole

    @pl.loop(0, members)
    def _(j):
        final_send[j] = resid_full[pl.ds(j, 1), :]

    def final_copy(to, slot):
        return remote(
            final_send.at[to], final_recv.at[slot], f_send.at[to], f_recv.at[slot], to
        )

    @pl.loop(1, members)
    def _(d):
        final_copy(peer(d), me).start()

    final_recv[me] = final_send[me]

    @pl.loop(1, members)
    def _(d):
        final_copy(me, peer(d)).wait_recv()

    for j in range(MSPLIT):
        line = final_recv[j * hsplit]
        for k in range(1, hsplit):
            line = line + final_recv[j * hsplit + k]
        out[:, j * block : (j + 1) * block] = line.astype(bf16)

    @pl.loop(1, members)
    def _(d):
        to = peer(d)
        stream_copy(to, me).wait_send()
        sq_copy(to, me).wait_send()
        final_copy(to, me).wait_send()

    @pl.loop(1, hsplit)
    def _(d):
        resid_copy(mate(d), h).wait_send()

    @pl.loop(0, MSPLIT)
    def _(i):
        @pl.loop(1, hsplit)
        def _(d):
            attn_relay(i, mate(d), me).wait_send()

    @pl.loop(1, MSPLIT)
    def _(d):
        attn_copy(d, me).wait_send()
        part_copy(model(d), m).wait_send()

    hid_copy(1, m).wait_send()

    @pl.loop(1, MSPLIT // 2)
    def _(j):
        hid_copy(2 * j, m).wait_send()
        hid_relay(j, m).wait_send()


def on_device(
    stream_in,
    query,
    key_new,
    value_new,
    key_cache,
    value_cache,
    lengths,
    route_ids,
    route_scores,
    out_weight,
    norm_gain,
    gate_weight,
    up_weight,
    down_weight,
):
    f32, bf16 = jnp.float32, jnp.bfloat16
    members = lax.axis_size("gx")
    width = stream_in.shape[1]
    hsplit = members // MSPLIT
    cols = width // members
    block = width // MSPLIT
    batch = members
    hidden_cols = gate_weight.shape[2]
    narrow = hidden_cols // MSPLIT
    chunk = narrow if narrow % 128 == 0 else hidden_cols
    ring = min(RING, hidden_cols // chunk)
    vmem = pl.BlockSpec(memory_space=pltpu.VMEM)
    smem = pl.BlockSpec(memory_space=pltpu.SMEM)
    hbm = pl.BlockSpec(memory_space=pl.ANY)
    dma = pltpu.SemaphoreType.DMA
    rows = key_cache.shape[1]
    cap = batch * 5 // 8
    packed = 2 * RESIDENT * cap
    shifts = [q * cap % 8 for q in range(4)]
    lead = (cap + max(shifts) + 7) // 8 * 8
    hid_rows = (RESIDENT * cap + 7) // 8 * 8
    lanes = (batch + 127) // 128 * 128
    return pl.pallas_call(
        functools.partial(kernel, members),
        out_shape=jax.ShapeDtypeStruct((1, width), bf16),
        in_specs=[vmem] * 3 + [hbm] * 2 + [smem] * 3 + [vmem] * 2 + [hbm] * 4,
        out_specs=vmem,
        scratch_shapes=[
            pltpu.VMEM((rows, KVH * HS), bf16),
            pltpu.VMEM((rows, KVH * HS), bf16),
            dma((2,)),
            pltpu.VMEM((NH, HS), f32),
            pltpu.VMEM((2, KVH, HS), f32),
            pltpu.VMEM((members, 1, cols), f32),
            pltpu.VMEM(out_weight.shape, bf16),
            pltpu.VMEM((ring, 4, block, chunk), bf16),
            pltpu.VMEM((MSPLIT, RESIDENT, narrow, block), bf16),
            pltpu.VMEM((NH + PAD, HS), bf16),
            pltpu.VMEM((members, NH + PAD, HS), bf16),
            pltpu.VMEM((members * (NH + PAD), HS), f32),
            pltpu.VMEM((batch, NH * HS), bf16),
            pltpu.VMEM((members, 1, cols), f32),
            pltpu.VMEM((hsplit, batch, cols), f32),
            pltpu.VMEM((batch, cols), f32),
            pltpu.VMEM((1, lanes), f32),
            pltpu.VMEM((members, 1, lanes), f32),
            pltpu.VMEM((batch, block), bf16),
            pltpu.VMEM((4, lead, block), bf16),
            pltpu.VMEM((packed + 8, chunk), f32),
            pltpu.VMEM((MSPLIT, packed, narrow), bf16),
            pltpu.VMEM((MSPLIT, packed, narrow), bf16),
            pltpu.VMEM((hid_rows, narrow), bf16),
            pltpu.VMEM((MSPLIT, hid_rows, narrow), bf16),
            pltpu.VMEM((RESIDENT, hid_rows, block), f32),
            pltpu.VMEM((batch, block), f32),
            pltpu.VMEM((members, 1, block), f32),
            pltpu.VMEM((members, 1, block), f32),
            dma,
            dma((ring, 4)),
            dma((MSPLIT, RESIDENT)),
        ]
        + [dma((MSPLIT,)), dma((MSPLIT, hsplit))]
        + [dma((members,))] * 5
        + [dma((hsplit,))] * 2
        + [dma((MSPLIT,))] * 5
        + [dma((members,))] * 2,
        compiler_params=pltpu.CompilerParams(
            collective_id=0, has_side_effects=True, vmem_limit_bytes=67043328
        ),
    )(
        query,
        key_new,
        value_new,
        key_cache.reshape(rows, KVH * HS),
        value_cache.reshape(rows, KVH * HS),
        lengths,
        route_ids,
        route_scores,
        stream_in,
        norm_gain.reshape(MSPLIT, 1, block),
        out_weight,
        gate_weight,
        up_weight,
        down_weight,
    )


def solution(mesh):
    return jax.shard_map(
        on_device,
        mesh=mesh,
        in_specs=(
            P(("groups", "gx"), None),
            P(("groups", "gx"), None),
            P(("groups", "gx"), None),
            P(("groups", "gx"), None),
            P(("groups", "gx"), None, None),
            P(("groups", "gx"), None, None),
            P(("groups", "gx")),
            P(("groups", "gx"), None),
            P(("groups", "gx"), None),
            P(None, "gx"),
            P(),
            P(None, "gx", None),
            P(None, "gx", None),
            P(None, "gx", None),
        ),
        out_specs=P(("groups", "gx"), None),
        check_vma=False,
    )
```

profile of v0, /device:TPU:0, one launch (start us, length us, event | category | flops | bytes accessed | tf_op | source)
XLA Modules:
  0.0 61.2 jit_solution(2054046778518560438)
XLA Ops:
  0.7 59.1 %shard_map.136 = bf16[1,8192]{1,0:T(2,128)(2,1)} custom-call(bf16[1,8192]{1,0:T(2,128)(2,1)} %query.1, bf16[1,1024]{1,0:T(2,128)(2,1)} %key_new.1, bf16[1,1024]{1,0:T(2,128)(2,1)} %value_new.1, bf16[128,1024]{1,0:T(8,128)(2,1)} %bitcast.3, bf16[128,1024]{1,0:T(8,128)(2,1)} %bitcast.4, s32[1]{0:T(128)S(6)} %copy.16.lengths, s32[1,2]{1,0:T(1,128)} %route_ids.1, ...), custom_call_target="tpu_custom_call" | custom-call | tf_op jit(solution)/shard_map/pallas_call | solution.py:567
  59.8 1.4 %copy.17 = bf16[1,8192]{1,0:T(2,128)(2,1)} copy(bf16[1,8192]{1,0:T(2,128)(2,1)} %shard_map.136) | data formatting | bytes 32768
where the time goes:
time: 61.4 us; the launch traced here: 61.2 us
  Pallas kernels  59.1 us (96%)
  local copies, waits for them, and re-layouts  1.41 us (2%)
  between operations  0.66 us (1%)
    pallas_call x1, Pallas kernels, on_device(): pl.pallas_call(functools.partial(kernel, members), out_shape=jax.ShapeDty...  59.1 us
    unnamed x1, local copies, waits for them, and re-layouts  1.41 us

commit v1 on v0

--- a/solution.py
+++ b/solution.py
@@ -18,7 +18,684 @@
 MESH = pl.DeviceIdType.MESH
 
 
-def kernel(
+QUADS = 7
+
+
+def large_kernel(
+    members,
+    query_hbm,
+    key_new_hbm,
+    value_new_hbm,
+    key_hbm,
+    value_hbm,
+    lengths,
+    route_ids,
+    route_scores,
+    stream_hbm,
+    gain_hbm,
+    out_weight,
+    gate_weight,
+    up_weight,
+    down_weight,
+    out,
+    query,
+    key_new,
+    value_new,
+    stream,
+    gain,
+    key_cache,
+    value_cache,
+    in_sem,
+    heads,
+    own_rows,
+    stream_rows,
+    stream_recv,
+    stream_flat,
+    pool,
+    attn_send,
+    attn_recv,
+    attn_wide,
+    attn_rows,
+    resid_keep,
+    y_send,
+    y_recv,
+    sq_send,
+    sq_recv,
+    slots_in,
+    acc,
+    px_send,
+    px_recv,
+    pz_send,
+    pz_recv,
+    hid_send,
+    hid_recv,
+    total,
+    final_flat,
+    final_send,
+    final_recv,
+    wo_sem,
+    gu_sem,
+    down_sem,
+    a_send,
+    a_relay,
+    a_recv,
+    s_send,
+    s_recv,
+    q_send,
+    q_recv,
+    r_send,
+    r_recv,
+    x_send,
+    x_recv,
+    z_send,
+    z_recv,
+    h_send,
+    h_relay,
+    h_recv,
+    f_send,
+    f_recv,
+):
+    f32, bf16 = jnp.float32, jnp.bfloat16
+    hsplit = members // MSPLIT
+    me = lax.axis_index("gx")
+    m = me // hsplit
+    h = lax.rem(me, hsplit)
+    batch = members
+    cols = y_send.shape[1]
+    width = cols * members
+    block = width // MSPLIT
+    group = NH // KVH
+    chunk = acc.shape[1]
+    cap = batch * 5 // 8
+    packed = px_send.shape[1]
+    hid_rows = hid_send.shape[0]
+    lead = slots_in.shape[1]
+    lanes = sq_send.shape[1]
+    half = MSPLIT // 2
+    side = block // cols
+    pieces = NH * HS // block
+
+    def peer(d):
+        return lax.rem(me + d, members)
+
+    def model(d):
+        d = jnp.asarray(d, jnp.int32)
+        to = 0
+        for b in (1, 2, 4):
+            to = to + lax.rem(lax.div(m, b) + lax.div(d, b), 2) * b
+        return to
+
+    def mate(d):
+        return lax.rem(h + d, hsplit)
+
+    def remote(src, dst, send, recv, device):
+        return pltpu.make_async_remote_copy(
+            src_ref=src,
+            dst_ref=dst,
+            send_sem=send,
+            recv_sem=recv,
+            device_id={"gx": device},
+            device_id_type=MESH,
+        )
+
+    barrier = pltpu.get_barrier_semaphore()
+
+    @pl.loop(1, members)
+    def _(d):
+        pl.semaphore_signal(barrier, inc=1, device_id={"gx": peer(d)}, device_id_type=MESH)
+
+    inputs = [
+        pltpu.make_async_copy(src, dst, in_sem.at[k])
+        for k, (src, dst) in enumerate(
+            (
+                (stream_hbm, stream),
+                (query_hbm, query),
+                (key_new_hbm, key_new),
+                (value_new_hbm, value_new),
+                (key_hbm, key_cache),
+                (value_hbm, value_cache),
+                (gain_hbm.at[me], gain),
+            )
+        )
+    ]
+    for copy in inputs:
+        copy.start()
+
+    def wo_copy(k):
+        return pltpu.make_async_copy(
+            out_weight.at[pl.ds(k * block, block), :],
+            pool.at[0, k // side, :, pl.ds(k % side * cols, cols)],
+            wo_sem.at[k],
+        )
+
+    def order(i):
+        return jnp.where(i < half, MSPLIT - 1 - 2 * i, 2 * (MSPLIT - 1 - i))
+
+    def gu_copy(i, q):
+        r, w = q // 2, (gate_weight, up_weight)[q % 2]
+        at = pl.multiple_of(model(order(i)) * chunk, 128)
+        return pltpu.make_async_copy(
+            w.at[r, :, pl.ds(at, chunk)],
+            pool.at[lax.rem(i + 1, QUADS), q, :, pl.ds(0, chunk)],
+            gu_sem.at[i, q],
+        )
+
+    def down_order(k):
+        return jnp.where(k < half, 2 * k, 2 * (k - half) + 1)
+
+    def down_slot(k, r):
+        return pool.at[2 + k // 2, k % 2 * 2 + r, pl.ds(0, chunk), :]
+
+    def down_copy(k, r):
+        at = pl.multiple_of(model(down_order(k)) * chunk, 16)
+        return pltpu.make_async_copy(
+            down_weight.at[r, pl.ds(at, chunk), :], down_slot(k, r), down_sem.at[k, r]
+        )
+
+    def down_pair(k):
+        for j in range(2):
+            for r in range(RESIDENT):
+                down_copy(2 * k + j, r).start()
+
+    for k in range(pieces):
+        wo_copy(k).start()
+
+    @pl.loop(0, QUADS - 1)
+    def _(i):
+        for q in range(4):
+            gu_copy(i, q).start()
+
+    scale = HS ** (-0.5)
+    spot = lax.broadcasted_iota(jnp.int32, (1, HS), 1)
+    full = lambda v: jnp.full((1, HS), v)
+    s0, s1 = full(route_scores[0, 0]), full(route_scores[0, 1])
+    i0, i1 = full(route_ids[0, 0]), full(route_ids[0, 1])
+    peak = jnp.maximum(s0, s1)
+    x0, x1 = jnp.exp(s0 - peak), jnp.exp(s1 - peak)
+    pick = jnp.where(i0 == spot, x0 / (x0 + x1), 0.0) + jnp.where(i1 == spot, x1 / (x0 + x1), 0.0)
+    pick = pick.astype(bf16).astype(f32)
+    inputs[0].wait()
+    for j in range(members):
+        stream_rows[j, :, :cols] = stream[:, j * cols : (j + 1) * cols].astype(f32)
+        stream_rows[j, :, cols:] = pick
+    for copy in inputs[1:4]:
+        copy.wait()
+    for n in range(NH):
+        heads[n : n + 1, :] = query[:, n * HS : (n + 1) * HS].astype(f32)
+    for g in range(KVH):
+        own_rows[0, g : g + 1, :] = key_new[:, g * HS : (g + 1) * HS].astype(f32)
+        own_rows[1, g : g + 1, :] = value_new[:, g * HS : (g + 1) * HS].astype(f32)
+    wide_q = heads[...]
+    for copy in inputs[4:]:
+        copy.wait()
+    s = jnp.concatenate(
+        [
+            lax.dot_general(
+                wide_q[g * group : (g + 1) * group].astype(bf16),
+                key_cache[:, g * HS : (g + 1) * HS],
+                (((1,), (1,)), ((), ())),
+                preferred_element_type=f32,
+            )
+            for g in range(KVH)
+        ],
+        axis=0,
+    )
+    s = s * scale
+    live = lax.broadcasted_iota(jnp.int32, s.shape, 1) < lengths[0]
+    s = jnp.where(live, s, -1e30)
+    k_own, v_own = own_rows[0], own_rows[1]
+    spread = lambda v: jnp.concatenate(
+        [jnp.broadcast_to(v[g : g + 1], (group, HS)) for g in range(KVH)], axis=0
+    )
+    own = jnp.sum(wide_q * spread(k_own), axis=-1, keepdims=True) * scale
+    top = jnp.maximum(jnp.max(s, axis=-1, keepdims=True), own)
+    e_cache = jnp.exp(s - top)
+    e_own = jnp.exp(own - top)
+    norm = jnp.sum(e_cache, axis=-1, keepdims=True) + e_own
+    p = e_cache / norm
+    p_own = (e_own / norm).astype(bf16).astype(f32)
+    mixed = jnp.concatenate(
+        [
+            jnp.dot(
+                p[g * group : (g + 1) * group].astype(bf16),
+                value_cache[:, g * HS : (g + 1) * HS],
+                preferred_element_type=f32,
+            )
+            for g in range(KVH)
+        ],
+        axis=0,
+    )
+    mixed = mixed + p_own * spread(v_own)
+    attn_send[...] = mixed.astype(bf16)
+
+    pl.semaphore_wait(barrier, members - 1)
+
+    def attn_copy(d, slot):
+        return remote(
+            attn_send, attn_recv.at[slot], a_send.at[d], a_recv.at[slot], model(d) * hsplit + h
+        )
+
+    def attn_relay(d, t, slot):
+        src = attn_send if isinstance(d, int) else attn_recv.at[slot]
+        return remote(
+            src, attn_recv.at[slot], a_relay.at[d, t], a_recv.at[slot], m * hsplit + t
+        )
+
+    def stream_copy(to, slot):
+        return remote(
+            stream_rows.at[to], stream_recv.at[slot], s_send.at[to], s_recv.at[slot], to
+        )
+
+    @pl.loop(0, MSPLIT - 1)
+    def _(i):
+        attn_copy(MSPLIT - 1 - i, me).start()
+
+    @pl.loop(1, hsplit)
+    def _(d):
+        attn_relay(0, mate(d), me).start()
+
+    @pl.loop(1, members)
+    def _(d):
+        stream_copy(peer(d), me).start()
+
+    def widen(slot, rows):
+        at = pl.multiple_of(slot * NH, NH)
+        attn_wide[pl.ds(at, NH), :] = rows.astype(f32)
+
+    widen(me, attn_send[...])
+    stream_recv[me] = stream_rows[me]
+
+    @pl.loop(1, MSPLIT)
+    def _(i):
+        slot = model(i) * hsplit + h
+        attn_copy(i, slot).wait_recv()
+
+        @pl.loop(1, hsplit)
+        def _(d):
+            attn_relay(i, mate(d), slot).start()
+
+        widen(slot, attn_recv[slot])
+
+    @pl.loop(1, members)
+    def _(d):
+        stream_copy(me, peer(d)).wait_recv()
+
+    for j in range(members):
+        stream_flat[j : j + 1, :] = stream_recv[j]
+
+    scales = [stream_flat[:, cols + r : cols + r + 1] for r in range(RESIDENT)]
+    sub = lax.broadcasted_iota(jnp.int32, (batch, batch), 0)
+    lane = lax.broadcasted_iota(jnp.int32, (batch, batch), 1)
+    named, rank, back = [], [], []
+    for r in range(RESIDENT):
+        col = jnp.where(scales[r] > 0.0, 1.0, 0.0)
+        row = jnp.sum(jnp.where(sub == lane, col, 0.0), axis=0, keepdims=True)
+        named.append(row)
+        rank.append(jnp.sum(jnp.where(sub < lane, col, 0.0), axis=0, keepdims=True))
+        place = jnp.sum(jnp.where(lane < sub, row, 0.0), axis=1, keepdims=True)
+        at = lax.broadcasted_iota(jnp.int32, (batch, hid_rows), 1)
+        hit = at == place.astype(jnp.int32) + r * cap
+        back.append(jnp.where(hit, scales[r], 0.0))
+
+    @pl.loop(0, MSPLIT)
+    def _(i):
+        @pl.loop(1, hsplit)
+        def _(d):
+            slot = model(i) * hsplit + mate(d)
+            attn_copy(i, slot).wait_recv()
+            widen(slot, attn_recv[slot])
+
+    for n in range(NH):
+        attn_rows[:, n * HS : (n + 1) * HS] = attn_wide[pl.ds(n, batch, stride=NH), :].astype(bf16)
+
+    for k in range(pieces):
+        wo_copy(k).wait()
+    proj = jnp.zeros((batch, cols), f32)
+    for k in range(pieces):
+        proj = proj + jnp.dot(
+            attn_rows[:, k * block : (k + 1) * block],
+            pool[0, k // side, :, k % side * cols : (k % side + 1) * cols],
+            preferred_element_type=f32,
+        )
+    for q in range(4):
+        gu_copy(QUADS - 1, q).start()
+
+    resid = stream_flat[:, :cols] + proj.astype(bf16).astype(f32)
+    resid_keep[...] = resid
+    y_send[...] = (resid * gain[...]).astype(bf16)
+
+    def y_copy(to, slot):
+        return remote(y_send, y_recv.at[slot], r_send.at[to], r_recv.at[slot], m * hsplit + to)
+
+    @pl.loop(1, hsplit)
+    def _(d):
+        y_copy(mate(d), h).start()
+
+    sub_w = lax.broadcasted_iota(jnp.int32, (batch, lanes), 0)
+    lane_w = lax.broadcasted_iota(jnp.int32, (batch, lanes), 1)
+    squares = jnp.sum(resid * resid, axis=-1, keepdims=True)
+    sq_send[...] = jnp.sum(jnp.where(sub_w == lane_w, squares, 0.0), axis=0, keepdims=True)
+
+    def sq_copy(to, slot):
+        return remote(sq_send, sq_recv.at[slot], q_send.at[to], q_recv.at[slot], to)
+
+    @pl.loop(1, members)
+    def _(d):
+        sq_copy(peer(d), me).start()
+
+    sq_recv[me] = sq_send[...]
+    y_recv[h] = y_send[...]
+
+    @pl.loop(1, hsplit)
+    def _(d):
+        y_copy(h, mate(d)).wait_recv()
+
+    y = jnp.concatenate([y_recv[j] for j in range(hsplit)], axis=1)
+    bases = [q * cap // 8 * 8 for q in range(4)]
+    for q in range(4):
+        r = q % 2
+        shift = q * cap - bases[q]
+        at = lax.broadcasted_iota(jnp.int32, (lead, batch), 0)
+        hit = (at == rank[r].astype(jnp.int32) + shift) & (named[r] > 0.0)
+        slots_in[q] = jnp.dot(
+            jnp.where(hit, 1.0, 0.0).astype(bf16), y, preferred_element_type=f32
+        ).astype(bf16)
+
+    def px_copy(i):
+        return remote(
+            px_send.at[i], px_recv.at[i], x_send.at[i], x_recv.at[i], model(1) * hsplit + h
+        )
+
+    def pz_copy(j):
+        return remote(
+            pz_send.at[j],
+            pz_recv.at[j],
+            z_send.at[j],
+            z_recv.at[j],
+            model(2 * (half - 1 - j)) * hsplit + h,
+        )
+
+    def sums(i):
+        acc[...] = jnp.zeros_like(acc)
+        for q in range(4):
+            gu_copy(i, q).wait()
+            acc[pl.ds(bases[ORDER[q]], lead), :] += jnp.dot(
+                slots_in[ORDER[q]],
+                pool[lax.rem(i + 1, QUADS), q, :, :chunk],
+                preferred_element_type=f32,
+            )
+
+    @pl.loop(0, half)
+    def _(i):
+        sums(i)
+        px_send[i] = acc[:packed, :].astype(bf16)
+        px_copy(i).start()
+
+        @pl.when(i == 0)
+        def _():
+            for q in range(4):
+                gu_copy(MSPLIT - 1, q).start()
+
+        @pl.when(i > 0)
+        def _():
+            down_pair(i - 1)
+
+    @pl.loop(half, MSPLIT)
+    def _(i):
+        sums(i)
+
+        @pl.when(i == half)
+        def _():
+            down_pair(half - 1)
+
+        px_copy(i - half).wait_recv()
+        acc[:packed, :] += px_recv[i - half].astype(f32)
+
+        @pl.when(i < MSPLIT - 1)
+        def _():
+            pz_send[i - half] = acc[:packed, :].astype(bf16)
+            pz_copy(i - half).start()
+
+    @pl.loop(1, members)
+    def _(d):
+        sq_copy(me, peer(d)).wait_recv()
+
+    power = jnp.sum(sq_recv[...], axis=0)[:, :batch] * (1.0 / width)
+    inverse = lax.rsqrt(power + 1e-05)
+    at = lax.broadcasted_iota(jnp.int32, (hid_rows, batch), 0)
+    scaled = jnp.zeros((hid_rows, 1), f32)
+    for r in range(RESIDENT):
+        hit = (at == rank[r].astype(jnp.int32) + r * cap) & (named[r] > 0.0)
+        scaled = scaled + jnp.sum(jnp.where(hit, inverse, 0.0), axis=1, keepdims=True)
+
+    for j in range(half - 1):
+        pz_copy(j).wait_recv()
+        acc[:packed, :] += pz_recv[j].astype(f32)
+    a = acc[:hid_rows, :] * scaled
+    b = acc[2 * cap : 2 * cap + hid_rows, :] * scaled
+    hid_send[...] = (a / (1.0 + jnp.exp(-a)) * b).astype(bf16)
+
+    def hid_copy(d, slot):
+        return remote(
+            hid_send, hid_recv.at[slot], h_send.at[d], h_recv.at[slot], model(d) * hsplit + h
+        )
+
+    def hid_relay(j, slot):
+        return remote(
+            hid_recv.at[slot],
+            hid_recv.at[slot],
+            h_relay.at[j],
+            h_recv.at[slot],
+            model(1) * hsplit + h,
+        )
+
+    hid_copy(1, m).start()
+
+    @pl.loop(1, half)
+    def _(j):
+        hid_copy(MSPLIT - 2 * j, m).start()
+
+    hid_recv[m] = hid_send[...]
+    total[...] = jnp.zeros_like(total)
+
+    @pl.loop(0, MSPLIT)
+    def _(k):
+        d = down_order(k)
+        slot = model(d)
+
+        @pl.when(k > 0)
+        def _():
+            hid_copy(d, slot).wait_recv()
+
+        @pl.when((k > 0) & (k < half))
+        def _():
+            hid_relay(k, slot).start()
+
+        for r in range(RESIDENT):
+            down_copy(k, r).wait()
+            total[r] += jnp.dot(
+                hid_recv[slot],
+                pool[2 + k // 2, k % 2 * 2 + r, :chunk, :],
+                preferred_element_type=f32,
+            )
+
+    resid = resid_keep[...]
+    whole = jnp.concatenate([jnp.where(h == j, resid, 0.0) for j in range(hsplit)], axis=1)
+    for r in range(RESIDENT):
+        for n in range(r * cap, (r + 1) * cap):
+            whole = whole + back[r][:, n : n + 1] * total[r, n : n + 1, :]
+    tiles = block // HS
+    for t in range(tiles):
+        final_flat[t * batch : (t + 1) * batch, :] = whole[:, t * HS : (t + 1) * HS]
+    for j in range(members):
+        final_send[j] = final_flat[pl.ds(j, tiles, stride=batch), :].astype(bf16)
+
+    def final_copy(to, slot):
+        return remote(
+            final_send.at[to], final_recv.at[slot], f_send.at[to], f_recv.at[slot], to
+        )
+
+    @pl.loop(1, members)
+    def _(d):
+        final_copy(peer(d), me).start()
+
+    final_recv[me] = final_send[me]
+
+    @pl.loop(1, members)
+    def _(d):
+        to = peer(d)
+        stream_copy(to, me).wait_send()
+        sq_copy(to, me).wait_send()
+
+    @pl.loop(1, hsplit)
+    def _(d):
+        y_copy(mate(d), h).wait_send()
+
+    @pl.loop(0, MSPLIT)
+    def _(i):
+        @pl.loop(1, hsplit)
+        def _(d):
+            attn_relay(i, mate(d), me).wait_send()
+
+    @pl.loop(1, MSPLIT)
+    def _(d):
+        attn_copy(d, me).wait_send()
+
+    for i in range(half):
+        px_copy(i).wait_send()
+    for j in range(half - 1):
+        pz_copy(j).wait_send()
+    hid_copy(1, m).wait_send()
+    for j in range(1, half):
+        hid_copy(2 * j, m).wait_send()
+        hid_relay(j, m).wait_send()
+
+    @pl.loop(1, members)
+    def _(d):
+        final_copy(me, peer(d)).wait_recv()
+
+    for j in range(MSPLIT):
+        line = final_recv[j * hsplit].astype(f32)
+        for k in range(1, hsplit):
+            line = line + final_recv[j * hsplit + k].astype(f32)
+        out[j * tiles : (j + 1) * tiles, :] = line.astype(bf16)
+
+    @pl.loop(1, members)
+    def _(d):
+        final_copy(peer(d), me).wait_send()
+
+
+def large_call(
+    stream_in,
+    query,
+    key_new,
+    value_new,
+    key_cache,
+    value_cache,
+    lengths,
+    route_ids,
+    route_scores,
+    out_weight,
+    norm_gain,
+    gate_weight,
+    up_weight,
+    down_weight,
+):
+    f32, bf16 = jnp.float32, jnp.bfloat16
+    members = lax.axis_size("gx")
+    width = stream_in.shape[1]
+    hsplit = members // MSPLIT
+    cols = width // members
+    block = width // MSPLIT
+    batch = members
+    narrow = gate_weight.shape[2] // MSPLIT
+    vmem = pl.BlockSpec(memory_space=pltpu.VMEM)
+    smem = pl.BlockSpec(memory_space=pltpu.SMEM)
+    hbm = pl.BlockSpec(memory_space=pl.ANY)
+    dma = pltpu.SemaphoreType.DMA
+    rows = key_cache.shape[1]
+    cap = batch * 5 // 8
+    packed = 2 * RESIDENT * cap
+    shifts = [q * cap % 8 for q in range(4)]
+    lead = (cap + max(shifts) + 7) // 8 * 8
+    hid_rows = (RESIDENT * cap + 7) // 8 * 8
+    lanes = (batch + 127) // 128 * 128
+    half = MSPLIT // 2
+    tiles = block // HS
+    result = pl.pallas_call(
+        functools.partial(large_kernel, members),
+        out_shape=jax.ShapeDtypeStruct((width // HS, HS), bf16),
+        in_specs=[hbm] * 5 + [smem] * 3 + [hbm] * 6,
+        out_specs=vmem,
+        scratch_shapes=[
+            pltpu.VMEM((1, NH * HS), bf16),
+            pltpu.VMEM((1, KVH * HS), bf16),
+            pltpu.VMEM((1, KVH * HS), bf16),
+            pltpu.VMEM((1, width), bf16),
+            pltpu.VMEM((1, cols), f32),
+            pltpu.VMEM((rows, KVH * HS), bf16),
+            pltpu.VMEM((rows, KVH * HS), bf16),
+            dma((7,)),
+            pltpu.VMEM((NH, HS), f32),
+            pltpu.VMEM((2, KVH, HS), f32),
+            pltpu.VMEM((members, 1, cols + HS), f32),
+            pltpu.VMEM((members, 1, cols + HS), f32),
+            pltpu.VMEM((batch, cols + HS), f32),
+            pltpu.VMEM((QUADS, 4, block, block), bf16),
+            pltpu.VMEM((NH, HS), bf16),
+            pltpu.VMEM((members, NH, HS), bf16),
+            pltpu.VMEM((members * NH, HS), f32),
+            pltpu.VMEM((batch, NH * HS), bf16),
+            pltpu.VMEM((batch, cols), f32),
+            pltpu.VMEM((batch, cols), bf16),
+            pltpu.VMEM((hsplit, batch, cols), bf16),
+            pltpu.VMEM((1, lanes), f32),
+            pltpu.VMEM((members, 1, lanes), f32),
+            pltpu.VMEM((4, lead, block), bf16),
+            pltpu.VMEM((packed + 8, narrow), f32),
+            pltpu.VMEM((half, packed, narrow), bf16),
+            pltpu.VMEM((half, packed, narrow), bf16),
+            pltpu.VMEM((half - 1, packed, narrow), bf16),
+            pltpu.VMEM((half - 1, packed, narrow), bf16),
+            pltpu.VMEM((hid_rows, narrow), bf16),
+            pltpu.VMEM((MSPLIT, hid_rows, narrow), bf16),
+            pltpu.VMEM((RESIDENT, hid_rows, block), f32),
+            pltpu.VMEM((tiles * batch, HS), f32),
+            pltpu.VMEM((members, tiles, HS), bf16),
+            pltpu.VMEM((members, tiles, HS), bf16),
+            dma((NH * HS // block,)),
+            dma((MSPLIT, 4)),
+            dma((MSPLIT, RESIDENT)),
+        ]
+        + [dma((MSPLIT,)), dma((MSPLIT, hsplit))]
+        + [dma((members,))] * 5
+        + [dma((hsplit,))] * 2
+        + [dma((half,))] * 4
+        + [dma((MSPLIT,)), dma((half,)), dma((MSPLIT,))]
+        + [dma((members,))] * 2,
+        compiler_params=pltpu.CompilerParams(
+            collective_id=0, has_side_effects=True, vmem_limit_bytes=67043328
+        ),
+    )(
+        query,
+        key_new,
+        value_new,
+        key_cache.reshape(rows, KVH * HS),
+        value_cache.reshape(rows, KVH * HS),
+        lengths,
+        route_ids,
+        route_scores,
+        stream_in,
+        norm_gain.reshape(members, 1, cols),
+        out_weight,
+        gate_weight,
+        up_weight,
+        down_weight,
+    )
+    return result.reshape(1, width)
+
+
+def small_kernel(
     members,
     query,
     key_new,
@@ -564,8 +1241,25 @@
     lead = (cap + max(shifts) + 7) // 8 * 8
     hid_rows = (RESIDENT * cap + 7) // 8 * 8
     lanes = (batch + 127) // 128 * 128
+    if narrow % 128 == 0 and narrow <= block and NH * HS * cols == 4 * block * block:
+        return large_call(
+            stream_in,
+            query,
+            key_new,
+            value_new,
+            key_cache,
+            value_cache,
+            lengths,
+            route_ids,
+            route_scores,
+            out_weight,
+            norm_gain,
+            gate_weight,
+            up_weight,
+            down_weight,
+        )
     return pl.pallas_call(
-        functools.partial(kernel, members),
+        functools.partial(small_kernel, members),
         out_shape=jax.ShapeDtypeStruct((1, width), bf16),
         in_specs=[vmem] * 3 + [hbm] * 2 + [smem] * 3 + [vmem] * 2 + [hbm] * 4,
         out_specs=vmem,

time: 61.4 us -> 52.3 us (0.85)
  Pallas kernels: 59.1 us -> 50 us
    pallas_call x1, Pallas kernels: 59.1 us -> 50 us  [large_call(): pl.pallas_call(functools.partial(large_kernel, members), out_shape=jax.Sh...]
where the time goes in v1:
time: 52.3 us; the launch traced here: 52.1 us
  Pallas kernels  50 us (96%)
  local copies, waits for them, and re-layouts  1.36 us (3%)
  between operations  0.66 us (1%)
    pallas_call x1, Pallas kernels, large_call(): pl.pallas_call(functools.partial(large_kernel, members), out_shape=jax.Sh...  50 us
    unnamed x1, local copies, waits for them, and re-layouts  1.36 us

profile of v1, /device:TPU:0, one launch (start us, length us, event | category | flops | bytes accessed | tf_op | source)
XLA Modules:
  0.0 52.1 jit_solution(2692664488393423521)
XLA Ops:
  0.7 50.0 %shard_map.136 = bf16[64,128]{1,0:T(8,128)(2,1)} custom-call(bf16[1,8192]{1,0:T(2,128)(2,1)} %query_hbm.1, bf16[1,1024]{1,0:T(2,128)(2,1)} %key_new_hbm.1, bf16[1,1024]{1,0:T(2,128)(2,1)} %value_new_hbm.1, bf16[128,1024]{1,0:T(8,128)(2,1)} %bitcast.8, bf16[128,1024]{1,0:T(8,128)(2,1)} %bitcast.9, s32[1]{0:T(128)S(6)} %copy.18.lengths, s32[1,2]{1,0:T(1,128)} %route_ids.1, ...), custom_call_target="tpu_custom_call" | custom-call | tf_op jit(solution)/shard_map/pallas_call | solution.py:625
  50.7 1.4 %copy.17 = bf16[1,1,64,128]{3,1,2,0:T(2,128)(2,1)} copy(bf16[1,1,64,128]{3,2,1,0:T(8,128)(2,1)} %bitcast.10) | data formatting | bytes 32768

commit v2 on v1

--- a/solution.py
+++ b/solution.py
@@ -17,9 +17,10 @@
 ORDER = (0, 2, 1, 3)
 MESH = pl.DeviceIdType.MESH
 
-
-QUADS = 7
-
+SLOTS = 28
+STAGES = ((0, 0), (0, 1), (1, 0), (1, 1))
+RELAYED = (True, False)
+SPREAD = (0, 2, 6, 4, 1, 3, 7, 5)
 
 def large_kernel(
     members,
@@ -28,9 +29,9 @@
     value_new_hbm,
     key_hbm,
     value_hbm,
-    lengths,
-    route_ids,
-    route_scores,
+    lengths_hbm,
+    ids_hbm,
+    scores_hbm,
     stream_hbm,
     gain_hbm,
     out_weight,
@@ -38,6 +39,9 @@
     up_weight,
     down_weight,
     out,
+    lengths,
+    route_ids,
+    route_scores,
     query,
     key_new,
     value_new,
@@ -62,13 +66,20 @@
     sq_send,
     sq_recv,
     slots_in,
-    acc,
-    px_send,
-    px_recv,
-    pz_send,
-    pz_recv,
-    hid_send,
-    hid_recv,
+    acc_a,
+    acc_b,
+    px_send_a,
+    px_send_b,
+    px_recv_a,
+    px_recv_b,
+    pz_send_a,
+    pz_send_b,
+    pz_recv_a,
+    pz_recv_b,
+    hid_send_a,
+    hid_send_b,
+    hid_recv_a,
+    hid_recv_b,
     total,
     final_flat,
     final_send,
@@ -105,11 +116,16 @@
     width = cols * members
     block = width // MSPLIT
     group = NH // KVH
-    chunk = acc.shape[1]
+    acc, px_send, px_recv = (acc_a, acc_b), (px_send_a, px_send_b), (px_recv_a, px_recv_b)
+    pz_send, pz_recv = (pz_send_a, pz_send_b), (pz_recv_a, pz_recv_b)
+    hid_send, hid_recv = (hid_send_a, hid_send_b), (hid_recv_a, hid_recv_b)
+    wide = (acc_a.shape[2], acc_b.shape[2])
+    first = (0, wide[0])
+    chunk = wide[0] + wide[1]
     cap = batch * 5 // 8
-    packed = px_send.shape[1]
-    hid_rows = hid_send.shape[0]
-    lead = slots_in.shape[1]
+    packed = px_send_a.shape[1]
+    hid_rows = hid_send_a.shape[0]
+    lead = slots_in.shape[1] // 2
     lanes = sq_send.shape[1]
     half = MSPLIT // 2
     side = block // cols
@@ -139,21 +155,19 @@
         )
 
     barrier = pltpu.get_barrier_semaphore()
-
-    @pl.loop(1, members)
-    def _(d):
-        pl.semaphore_signal(barrier, inc=1, device_id={"gx": peer(d)}, device_id_type=MESH)
-
     inputs = [
         pltpu.make_async_copy(src, dst, in_sem.at[k])
         for k, (src, dst) in enumerate(
             (
-                (stream_hbm, stream),
                 (query_hbm, query),
+                (key_hbm, key_cache),
+                (value_hbm, value_cache),
                 (key_new_hbm, key_new),
                 (value_new_hbm, value_new),
-                (key_hbm, key_cache),
-                (value_hbm, value_cache),
+                (lengths_hbm, lengths),
+                (ids_hbm, route_ids),
+                (scores_hbm, route_scores),
+                (stream_hbm, stream),
                 (gain_hbm.at[me], gain),
             )
         )
@@ -161,73 +175,83 @@
     for copy in inputs:
         copy.start()
 
+    @pl.loop(1, members)
+    def _(d):
+        pl.semaphore_signal(barrier, inc=1, device_id={"gx": peer(d)}, device_id_type=MESH)
+
     def wo_copy(k):
         return pltpu.make_async_copy(
             out_weight.at[pl.ds(k * block, block), :],
-            pool.at[0, k // side, :, pl.ds(k % side * cols, cols)],
+            pool.at[k // side, :, pl.ds(k % side * cols, cols)],
             wo_sem.at[k],
         )
 
-    def order(i):
-        return jnp.where(i < half, MSPLIT - 1 - 2 * i, 2 * (MSPLIT - 1 - i))
-
-    def gu_copy(i, q):
+    def gu_slot(p, z, i, r):
+        return lax.rem(half + MSPLIT * STAGES.index((p, z)) + 2 * i + r, SLOTS)
+
+    def gu_copy(p, z, i, q):
         r, w = q // 2, (gate_weight, up_weight)[q % 2]
-        at = pl.multiple_of(model(order(i)) * chunk, 128)
+        at = pl.multiple_of(model(2 * (half - 1 - i) + 1 - z) * chunk + first[p], 128)
         return pltpu.make_async_copy(
-            w.at[r, :, pl.ds(at, chunk)],
-            pool.at[lax.rem(i + 1, QUADS), q, :, pl.ds(0, chunk)],
-            gu_sem.at[i, q],
-        )
+            w.at[r, :, pl.ds(at, wide[p])],
+            pool.at[gu_slot(p, z, i, r), :, pl.ds(q % 2 * wide[p], wide[p])],
+            gu_sem.at[p, z * half + i, q],
+        )
+
+    def gu_start(s, i):
+        for q in range(4):
+            gu_copy(*STAGES[s], i, q).start()
 
     def down_order(k):
-        return jnp.where(k < half, 2 * k, 2 * (k - half) + 1)
-
-    def down_slot(k, r):
-        return pool.at[2 + k // 2, k % 2 * 2 + r, pl.ds(0, chunk), :]
-
-    def down_copy(k, r):
-        at = pl.multiple_of(model(down_order(k)) * chunk, 16)
+        if isinstance(k, int):
+            return SPREAD[k]
+        d = 0
+        for j, to in enumerate(SPREAD):
+            d = d + jnp.where(k == j, to, 0)
+        return d
+
+    def down_slot(p, k):
+        return lax.rem(half + (4 + p) * MSPLIT + k, SLOTS)
+
+    def down_copy(p, k, r):
+        at = pl.multiple_of(model(down_order(k)) * chunk + first[p], 16)
         return pltpu.make_async_copy(
-            down_weight.at[r, pl.ds(at, chunk), :], down_slot(k, r), down_sem.at[k, r]
-        )
-
-    def down_pair(k):
+            down_weight.at[r, pl.ds(at, wide[p]), :],
+            pool.at[down_slot(p, k), pl.ds(r * wide[p], wide[p]), :],
+            down_sem.at[p, k, r],
+        )
+
+    def down_start(p, k):
         for j in range(2):
             for r in range(RESIDENT):
-                down_copy(2 * k + j, r).start()
+                down_copy(p, k + j, r).start()
+
+    def refill(p, z, i):
+        s = STAGES.index((p, z))
+        cases = (
+            (lambda: gu_start(3, i + 2), lambda: down_start(0, 2 * i - 4)),
+            (lambda: down_start(0, 2 * i + 4), lambda: down_start(1, 2 * i - 4)),
+            (lambda: down_start(1, 2 * i + 4),),
+            (),
+        )
+        for test, load in zip((i < 2, i >= 2), cases[s]):
+            pl.when(test)(load)
 
     for k in range(pieces):
         wo_copy(k).start()
 
-    @pl.loop(0, QUADS - 1)
-    def _(i):
-        for q in range(4):
-            gu_copy(i, q).start()
-
     scale = HS ** (-0.5)
-    spot = lax.broadcasted_iota(jnp.int32, (1, HS), 1)
-    full = lambda v: jnp.full((1, HS), v)
-    s0, s1 = full(route_scores[0, 0]), full(route_scores[0, 1])
-    i0, i1 = full(route_ids[0, 0]), full(route_ids[0, 1])
-    peak = jnp.maximum(s0, s1)
-    x0, x1 = jnp.exp(s0 - peak), jnp.exp(s1 - peak)
-    pick = jnp.where(i0 == spot, x0 / (x0 + x1), 0.0) + jnp.where(i1 == spot, x1 / (x0 + x1), 0.0)
-    pick = pick.astype(bf16).astype(f32)
     inputs[0].wait()
-    for j in range(members):
-        stream_rows[j, :, :cols] = stream[:, j * cols : (j + 1) * cols].astype(f32)
-        stream_rows[j, :, cols:] = pick
-    for copy in inputs[1:4]:
-        copy.wait()
     for n in range(NH):
         heads[n : n + 1, :] = query[:, n * HS : (n + 1) * HS].astype(f32)
+
+    for copy in inputs[1:]:
+        copy.wait()
+
     for g in range(KVH):
         own_rows[0, g : g + 1, :] = key_new[:, g * HS : (g + 1) * HS].astype(f32)
         own_rows[1, g : g + 1, :] = value_new[:, g * HS : (g + 1) * HS].astype(f32)
     wide_q = heads[...]
-    for copy in inputs[4:]:
-        copy.wait()
     s = jnp.concatenate(
         [
             lax.dot_general(
@@ -267,6 +291,17 @@
     )
     mixed = mixed + p_own * spread(v_own)
     attn_send[...] = mixed.astype(bf16)
+    spot = lax.broadcasted_iota(jnp.int32, (1, HS), 1)
+    full = lambda v: jnp.full((1, HS), v)
+    s0, s1 = full(route_scores[0, 0]), full(route_scores[0, 1])
+    i0, i1 = full(route_ids[0, 0]), full(route_ids[0, 1])
+    peak = jnp.maximum(s0, s1)
+    x0, x1 = jnp.exp(s0 - peak), jnp.exp(s1 - peak)
+    pick = jnp.where(i0 == spot, x0 / (x0 + x1), 0.0) + jnp.where(i1 == spot, x1 / (x0 + x1), 0.0)
+    pick = pick.astype(bf16).astype(f32)
+    for j in range(members):
+        stream_rows[j, :, :cols] = stream[:, j * cols : (j + 1) * cols].astype(f32)
+        stream_rows[j, :, cols:] = pick
 
     pl.semaphore_wait(barrier, members - 1)
 
@@ -301,6 +336,12 @@
     def widen(slot, rows):
         at = pl.multiple_of(slot * NH, NH)
         attn_wide[pl.ds(at, NH), :] = rows.astype(f32)
+
+    for s in range(3):
+
+        @pl.loop(0, half)
+        def _(i):
+            gu_start(s, i)
 
     widen(me, attn_send[...])
     stream_recv[me] = stream_rows[me]
@@ -316,6 +357,17 @@
 
         widen(slot, attn_recv[slot])
 
+    @pl.loop(0, MSPLIT)
+    def _(i):
+        @pl.loop(1, hsplit)
+        def _(d):
+            slot = model(i) * hsplit + mate(d)
+            attn_copy(i, slot).wait_recv()
+            widen(slot, attn_recv[slot])
+
+    for k in range(pieces):
+        wo_copy(k).wait()
+
     @pl.loop(1, members)
     def _(d):
         stream_copy(me, peer(d)).wait_recv()
@@ -323,6 +375,44 @@
     for j in range(members):
         stream_flat[j : j + 1, :] = stream_recv[j]
 
+    for n in range(NH):
+        attn_rows[:, n * HS : (n + 1) * HS] = attn_wide[pl.ds(n, batch, stride=NH), :].astype(bf16)
+
+    proj = jnp.zeros((batch, cols), f32)
+    for k in range(pieces):
+        proj = proj + jnp.dot(
+            attn_rows[:, k * block : (k + 1) * block],
+            pool[k // side, :, k % side * cols : (k % side + 1) * cols],
+            preferred_element_type=f32,
+        )
+    gu_start(3, 0)
+    gu_start(3, 1)
+
+    resid = stream_flat[:, :cols] + proj.astype(bf16).astype(f32)
+    resid_keep[...] = resid
+    y_send[...] = (resid * gain[...]).astype(bf16)
+
+    def y_copy(to, slot):
+        return remote(y_send, y_recv.at[slot], r_send.at[to], r_recv.at[slot], m * hsplit + to)
+
+    @pl.loop(1, hsplit)
+    def _(d):
+        y_copy(mate(d), h).start()
+
+    sub_w = lax.broadcasted_iota(jnp.int32, (batch, lanes), 0)
+    lane_w = lax.broadcasted_iota(jnp.int32, (batch, lanes), 1)
+    squares = jnp.sum(resid * resid, axis=-1, keepdims=True)
+    sq_send[...] = jnp.sum(jnp.where(sub_w == lane_w, squares, 0.0), axis=0, keepdims=True)
+
+    def sq_copy(to, slot):
+        return remote(sq_send, sq_recv.at[slot], q_send.at[to], q_recv.at[slot], to)
+
+    @pl.loop(1, members)
+    def _(d):
+        sq_copy(peer(d), me).start()
+
+    sq_recv[me] = sq_send[...]
+    y_recv[h] = y_send[...]
     scales = [stream_flat[:, cols + r : cols + r + 1] for r in range(RESIDENT)]
     sub = lax.broadcasted_iota(jnp.int32, (batch, batch), 0)
     lane = lax.broadcasted_iota(jnp.int32, (batch, batch), 1)
@@ -337,55 +427,6 @@
         hit = at == place.astype(jnp.int32) + r * cap
         back.append(jnp.where(hit, scales[r], 0.0))
 
-    @pl.loop(0, MSPLIT)
-    def _(i):
-        @pl.loop(1, hsplit)
-        def _(d):
-            slot = model(i) * hsplit + mate(d)
-            attn_copy(i, slot).wait_recv()
-            widen(slot, attn_recv[slot])
-
-    for n in range(NH):
-        attn_rows[:, n * HS : (n + 1) * HS] = attn_wide[pl.ds(n, batch, stride=NH), :].astype(bf16)
-
-    for k in range(pieces):
-        wo_copy(k).wait()
-    proj = jnp.zeros((batch, cols), f32)
-    for k in range(pieces):
-        proj = proj + jnp.dot(
-            attn_rows[:, k * block : (k + 1) * block],
-            pool[0, k // side, :, k % side * cols : (k % side + 1) * cols],
-            preferred_element_type=f32,
-        )
-    for q in range(4):
-        gu_copy(QUADS - 1, q).start()
-
-    resid = stream_flat[:, :cols] + proj.astype(bf16).astype(f32)
-    resid_keep[...] = resid
-    y_send[...] = (resid * gain[...]).astype(bf16)
-
-    def y_copy(to, slot):
-        return remote(y_send, y_recv.at[slot], r_send.at[to], r_recv.at[slot], m * hsplit + to)
-
-    @pl.loop(1, hsplit)
-    def _(d):
-        y_copy(mate(d), h).start()
-
-    sub_w = lax.broadcasted_iota(jnp.int32, (batch, lanes), 0)
-    lane_w = lax.broadcasted_iota(jnp.int32, (batch, lanes), 1)
-    squares = jnp.sum(resid * resid, axis=-1, keepdims=True)
-    sq_send[...] = jnp.sum(jnp.where(sub_w == lane_w, squares, 0.0), axis=0, keepdims=True)
-
-    def sq_copy(to, slot):
-        return remote(sq_send, sq_recv.at[slot], q_send.at[to], q_recv.at[slot], to)
-
-    @pl.loop(1, members)
-    def _(d):
-        sq_copy(peer(d), me).start()
-
-    sq_recv[me] = sq_send[...]
-    y_recv[h] = y_send[...]
-
     @pl.loop(1, hsplit)
     def _(d):
         y_copy(h, mate(d)).wait_recv()
@@ -397,64 +438,142 @@
         shift = q * cap - bases[q]
         at = lax.broadcasted_iota(jnp.int32, (lead, batch), 0)
         hit = (at == rank[r].astype(jnp.int32) + shift) & (named[r] > 0.0)
-        slots_in[q] = jnp.dot(
+        slots_in[r, q // 2 * lead : (q // 2 + 1) * lead, :] = jnp.dot(
             jnp.where(hit, 1.0, 0.0).astype(bf16), y, preferred_element_type=f32
         ).astype(bf16)
 
-    def px_copy(i):
-        return remote(
-            px_send.at[i], px_recv.at[i], x_send.at[i], x_recv.at[i], model(1) * hsplit + h
-        )
-
-    def pz_copy(j):
-        return remote(
-            pz_send.at[j],
-            pz_recv.at[j],
-            z_send.at[j],
-            z_recv.at[j],
+    def px_copy(p, i):
+        return remote(
+            px_send[p].at[i],
+            px_recv[p].at[i],
+            x_send.at[p, i],
+            x_recv.at[p, i],
+            model(1) * hsplit + h,
+        )
+
+    def pz_copy(p, j):
+        return remote(
+            pz_send[p].at[j],
+            pz_recv[p].at[j],
+            z_send.at[p, j],
+            z_recv.at[p, j],
             model(2 * (half - 1 - j)) * hsplit + h,
         )
 
-    def sums(i):
-        acc[...] = jnp.zeros_like(acc)
+    def sums(p, z, i):
+        w = wide[p]
+        slabs = [[] for _ in range(acc[p].shape[1] // 8)]
+        for r in range(RESIDENT):
+            where = gu_slot(p, z, i, r)
+            values = [
+                jnp.dot(
+                    slots_in[r, q * lead : (q + 1) * lead, :],
+                    pool[where, :, q * w : (q + 1) * w],
+                    preferred_element_type=f32,
+                )
+                for q in range(2)
+            ]
+            for q in range(2):
+                for k in range(lead // 8):
+                    slabs[bases[2 * q + r] // 8 + k].append(values[q][k * 8 : (k + 1) * 8])
+        empty = jnp.zeros((8, w), f32)
+        return jnp.concatenate([sum(slab[1:], slab[0]) if slab else empty for slab in slabs], axis=0)
+
+    def arrived(p, z, i):
         for q in range(4):
-            gu_copy(i, q).wait()
-            acc[pl.ds(bases[ORDER[q]], lead), :] += jnp.dot(
-                slots_in[ORDER[q]],
-                pool[lax.rem(i + 1, QUADS), q, :, :chunk],
+            gu_copy(p, z, i, q).wait()
+
+    def gu_x(p, pair):
+        @pl.loop(0, half, step=pair)
+        def _(i):
+            for j in range(pair):
+                arrived(p, 0, i + j)
+            for j in range(pair):
+                px_send[p][i + j] = sums(p, 0, i + j)[:packed].astype(bf16)
+            for j in range(pair):
+                px_copy(p, i + j).start()
+            for j in range(pair):
+                refill(p, 0, i + j)
+
+    def gu_z(p, pair):
+        @pl.loop(0, half, step=pair)
+        def _(i):
+            for j in range(pair):
+                arrived(p, 1, i + j)
+            for j in range(pair):
+                acc[p][j] = sums(p, 1, i + j)
+            for j in range(pair):
+                refill(p, 1, i + j)
+                px_copy(p, i + j).wait_recv()
+                acc[p][j, :packed, :] += px_recv[p][i + j].astype(f32)
+
+                @pl.when(i + j < half - 1)
+                def _():
+                    pz_send[p][i + j] = acc[p][j, :packed, :].astype(bf16)
+                    pz_copy(p, i + j).start()
+
+    def hid_copy(p, d, slot):
+        return remote(
+            hid_send[p],
+            hid_recv[p].at[slot],
+            h_send.at[p, d],
+            h_recv.at[p, slot],
+            model(d) * hsplit + h,
+        )
+
+    def hid_relay(p, j, slot):
+        return remote(
+            hid_recv[p].at[slot],
+            hid_recv[p].at[slot],
+            h_relay.at[p, j],
+            h_recv.at[p, slot],
+            model(1) * hsplit + h,
+        )
+
+    def finish(p, last):
+        for j in range(half - 1):
+            pz_copy(p, j).wait_recv()
+            acc[p][last, :packed, :] += pz_recv[p][j].astype(f32)
+        a = acc[p][last, :hid_rows, :] * scaled
+        b = acc[p][last, 2 * cap : 2 * cap + hid_rows, :] * scaled
+        hid_send[p][...] = (a / (1.0 + jnp.exp(-a)) * b).astype(bf16)
+        for d in (1, *SPREAD[1:half]) if RELAYED[p] else range(MSPLIT - 1, 0, -1):
+            hid_copy(p, d, m).start()
+        hid_recv[p][m] = hid_send[p][...]
+
+    def relays(p):
+        for k in range(1, half):
+            slot = model(SPREAD[k])
+            hid_copy(p, SPREAD[k], slot).wait_recv()
+            hid_relay(p, k, slot).start()
+
+    def down(p, ks, fresh=False):
+        for k in ks:
+            if k >= half or k and not RELAYED[p]:
+                hid_copy(p, SPREAD[k], model(SPREAD[k])).wait_recv()
+            for r in range(RESIDENT):
+                down_copy(p, k, r).wait()
+        line = lax.broadcasted_iota(jnp.int32, (hid_rows, wide[p]), 0)
+        value = None if fresh else total[...]
+        for k in ks:
+            rows = hid_recv[p][model(SPREAD[k])].astype(f32)
+            split = [
+                jnp.where((line >= r * cap) & (line < (r + 1) * cap), rows, 0.0).astype(bf16)
+                for r in range(RESIDENT)
+            ]
+            term = jnp.dot(
+                jnp.concatenate(split, axis=1),
+                pool[down_slot(p, k), : RESIDENT * wide[p], :],
                 preferred_element_type=f32,
             )
-
-    @pl.loop(0, half)
-    def _(i):
-        sums(i)
-        px_send[i] = acc[:packed, :].astype(bf16)
-        px_copy(i).start()
-
-        @pl.when(i == 0)
-        def _():
-            for q in range(4):
-                gu_copy(MSPLIT - 1, q).start()
-
-        @pl.when(i > 0)
-        def _():
-            down_pair(i - 1)
-
-    @pl.loop(half, MSPLIT)
-    def _(i):
-        sums(i)
-
-        @pl.when(i == half)
-        def _():
-            down_pair(half - 1)
-
-        px_copy(i - half).wait_recv()
-        acc[:packed, :] += px_recv[i - half].astype(f32)
-
-        @pl.when(i < MSPLIT - 1)
-        def _():
-            pz_send[i - half] = acc[:packed, :].astype(bf16)
-            pz_copy(i - half).start()
+            value = term if value is None else value + term
+        total[...] = value
+
+    gu_x(0, 1)
+
+    gu_z(0, 2)
+
+    gu_x(1, 2)
 
     @pl.loop(1, members)
     def _(d):
@@ -468,62 +587,29 @@
         hit = (at == rank[r].astype(jnp.int32) + r * cap) & (named[r] > 0.0)
         scaled = scaled + jnp.sum(jnp.where(hit, inverse, 0.0), axis=1, keepdims=True)
 
-    for j in range(half - 1):
-        pz_copy(j).wait_recv()
-        acc[:packed, :] += pz_recv[j].astype(f32)
-    a = acc[:hid_rows, :] * scaled
-    b = acc[2 * cap : 2 * cap + hid_rows, :] * scaled
-    hid_send[...] = (a / (1.0 + jnp.exp(-a)) * b).astype(bf16)
-
-    def hid_copy(d, slot):
-        return remote(
-            hid_send, hid_recv.at[slot], h_send.at[d], h_recv.at[slot], model(d) * hsplit + h
-        )
-
-    def hid_relay(j, slot):
-        return remote(
-            hid_recv.at[slot],
-            hid_recv.at[slot],
-            h_relay.at[j],
-            h_recv.at[slot],
-            model(1) * hsplit + h,
-        )
-
-    hid_copy(1, m).start()
-
-    @pl.loop(1, half)
-    def _(j):
-        hid_copy(MSPLIT - 2 * j, m).start()
-
-    hid_recv[m] = hid_send[...]
-    total[...] = jnp.zeros_like(total)
-
-    @pl.loop(0, MSPLIT)
-    def _(k):
-        d = down_order(k)
-        slot = model(d)
-
-        @pl.when(k > 0)
-        def _():
-            hid_copy(d, slot).wait_recv()
-
-        @pl.when((k > 0) & (k < half))
-        def _():
-            hid_relay(k, slot).start()
-
-        for r in range(RESIDENT):
-            down_copy(k, r).wait()
-            total[r] += jnp.dot(
-                hid_recv[slot],
-                pool[2 + k // 2, k % 2 * 2 + r, :chunk, :],
-                preferred_element_type=f32,
-            )
+    finish(0, 1)
+
+    gu_z(1, 1)
+
+    relays(0)
+
+    down(0, range(half), True)
+
+    finish(1, 0)
+
+    down(0, range(half, MSPLIT))
+
+    down(1, range(half))
+
+    down(1, (4, 5))
+
+    down(1, (6, 7))
 
     resid = resid_keep[...]
     whole = jnp.concatenate([jnp.where(h == j, resid, 0.0) for j in range(hsplit)], axis=1)
-    for r in range(RESIDENT):
-        for n in range(r * cap, (r + 1) * cap):
-            whole = whole + back[r][:, n : n + 1] * total[r, n : n + 1, :]
+    mix = sum(back[1:], back[0])
+    for n in range(RESIDENT * cap):
+        whole = whole + mix[:, n : n + 1] * total[n : n + 1, :]
     tiles = block // HS
     for t in range(tiles):
         final_flat[t * batch : (t + 1) * batch, :] = whole[:, t * HS : (t + 1) * HS]
@@ -561,14 +647,15 @@
     def _(d):
         attn_copy(d, me).wait_send()
 
-    for i in range(half):
-        px_copy(i).wait_send()
-    for j in range(half - 1):
-        pz_copy(j).wait_send()
-    hid_copy(1, m).wait_send()
-    for j in range(1, half):
-        hid_copy(2 * j, m).wait_send()
-        hid_relay(j, m).wait_send()
+    for p in range(2):
+        for i in range(half):
+            px_copy(p, i).wait_send()
+        for j in range(half - 1):
+            pz_copy(p, j).wait_send()
+        for d in (1, *SPREAD[1:half]) if RELAYED[p] else range(1, MSPLIT):
+            hid_copy(p, d, m).wait_send()
+        for j in range(1, half if RELAYED[p] else 1):
+            hid_relay(p, j, m).wait_send()
 
     @pl.loop(1, members)
     def _(d):
@@ -583,7 +670,6 @@
     @pl.loop(1, members)
     def _(d):
         final_copy(peer(d), me).wait_send()
-
 
 def large_call(
     stream_in,
@@ -610,7 +696,6 @@
     batch = members
     narrow = gate_weight.shape[2] // MSPLIT
     vmem = pl.BlockSpec(memory_space=pltpu.VMEM)
-    smem = pl.BlockSpec(memory_space=pltpu.SMEM)
     hbm = pl.BlockSpec(memory_space=pl.ANY)
     dma = pltpu.SemaphoreType.DMA
     rows = key_cache.shape[1]
@@ -622,12 +707,17 @@
     lanes = (batch + 127) // 128 * 128
     half = MSPLIT // 2
     tiles = block // HS
+    wide = [(narrow // 128 + 1) // 2 * 128]
+    wide.append(narrow - wide[0])
     result = pl.pallas_call(
         functools.partial(large_kernel, members),
-        out_shape=jax.ShapeDtypeStruct((width // HS, HS), bf16),
-        in_specs=[hbm] * 5 + [smem] * 3 + [hbm] * 6,
+        out_shape=pltpu.VMEM((width // HS, HS), bf16),
+        in_specs=[hbm] * 14,
         out_specs=vmem,
         scratch_shapes=[
+            pltpu.SMEM(lengths.shape, jnp.int32),
+            pltpu.SMEM(route_ids.shape, jnp.int32),
+            pltpu.SMEM(route_scores.shape, f32),
             pltpu.VMEM((1, NH * HS), bf16),
             pltpu.VMEM((1, KVH * HS), bf16),
             pltpu.VMEM((1, KVH * HS), bf16),
@@ -635,13 +725,13 @@
             pltpu.VMEM((1, cols), f32),
             pltpu.VMEM((rows, KVH * HS), bf16),
             pltpu.VMEM((rows, KVH * HS), bf16),
-            dma((7,)),
+            dma((10,)),
             pltpu.VMEM((NH, HS), f32),
             pltpu.VMEM((2, KVH, HS), f32),
             pltpu.VMEM((members, 1, cols + HS), f32),
             pltpu.VMEM((members, 1, cols + HS), f32),
             pltpu.VMEM((batch, cols + HS), f32),
-            pltpu.VMEM((QUADS, 4, block, block), bf16),
+            pltpu.VMEM((SLOTS, block, block), bf16),
             pltpu.VMEM((NH, HS), bf16),
             pltpu.VMEM((members, NH, HS), bf16),
             pltpu.VMEM((members * NH, HS), f32),
@@ -651,30 +741,30 @@
             pltpu.VMEM((hsplit, batch, cols), bf16),
             pltpu.VMEM((1, lanes), f32),
             pltpu.VMEM((members, 1, lanes), f32),
-            pltpu.VMEM((4, lead, block), bf16),
-            pltpu.VMEM((packed + 8, narrow), f32),
-            pltpu.VMEM((half, packed, narrow), bf16),
-            pltpu.VMEM((half, packed, narrow), bf16),
-            pltpu.VMEM((half - 1, packed, narrow), bf16),
-            pltpu.VMEM((half - 1, packed, narrow), bf16),
-            pltpu.VMEM((hid_rows, narrow), bf16),
-            pltpu.VMEM((MSPLIT, hid_rows, narrow), bf16),
-            pltpu.VMEM((RESIDENT, hid_rows, block), f32),
+            pltpu.VMEM((RESIDENT, 2 * lead, block), bf16),
+            *[pltpu.VMEM((2, packed + 8, w), f32) for w in wide],
+            *[pltpu.VMEM((half, packed, w), bf16) for w in wide],
+            *[pltpu.VMEM((half, packed, w), bf16) for w in wide],
+            *[pltpu.VMEM((half - 1, packed, w), bf16) for w in wide],
+            *[pltpu.VMEM((half - 1, packed, w), bf16) for w in wide],
+            *[pltpu.VMEM((hid_rows, w), bf16) for w in wide],
+            *[pltpu.VMEM((MSPLIT, hid_rows, w), bf16) for w in wide],
+            pltpu.VMEM((hid_rows, block), f32),
             pltpu.VMEM((tiles * batch, HS), f32),
             pltpu.VMEM((members, tiles, HS), bf16),
             pltpu.VMEM((members, tiles, HS), bf16),
             dma((NH * HS // block,)),
-            dma((MSPLIT, 4)),
-            dma((MSPLIT, RESIDENT)),
+            dma((2, MSPLIT, 4)),
+            dma((2, MSPLIT, RESIDENT)),
         ]
         + [dma((MSPLIT,)), dma((MSPLIT, hsplit))]
         + [dma((members,))] * 5
         + [dma((hsplit,))] * 2
-        + [dma((half,))] * 4
-        + [dma((MSPLIT,)), dma((half,)), dma((MSPLIT,))]
+        + [dma((2, half))] * 4
+        + [dma((2, MSPLIT)), dma((2, half)), dma((2, MSPLIT))]
         + [dma((members,))] * 2,
         compiler_params=pltpu.CompilerParams(
-            collective_id=0, has_side_effects=True, vmem_limit_bytes=67043328
+            collective_id=0, has_side_effects=True, vmem_limit_bytes=66000000
         ),
     )(
         query,
@@ -693,7 +783,6 @@
         down_weight,
     )
     return result.reshape(1, width)
-
 
 def small_kernel(
     members,
@@ -1202,7 +1291,6 @@
         hid_copy(2 * j, m).wait_send()
         hid_relay(j, m).wait_send()
 
-
 def on_device(
     stream_in,
     query,
@@ -1241,7 +1329,7 @@
     lead = (cap + max(shifts) + 7) // 8 * 8
     hid_rows = (RESIDENT * cap + 7) // 8 * 8
     lanes = (batch + 127) // 128 * 128
-    if narrow % 128 == 0 and narrow <= block and NH * HS * cols == 4 * block * block:
+    if narrow % 128 == 0 and 256 <= narrow <= block and NH * HS * cols == 4 * block * block:
         return large_call(
             stream_in,
             query,
@@ -1322,7 +1410,6 @@
         down_weight,
     )
 
-
 def solution(mesh):
     return jax.shard_map(
         on_device,

time: 52.3 us -> 45.3 us (0.87)
  Pallas kernels: 50 us -> 43.8 us
  local copies, waits for them, and re-layouts: 1.36 us -> 0.64 us
    pallas_call x1, Pallas kernels: 50 us -> 43.8 us  [large_call(): pl.pallas_call(functools.partial(large_kernel, members), out_shape=pltpu....]
    unnamed x1, local copies, waits for them, and re-layouts: 1.36 us -> 0.64 us
where the time goes in v2:
time: 45.3 us; the launch traced here: 45.1 us
  Pallas kernels  43.8 us (97%)
  between operations  0.66 us (1%)
  local copies, waits for them, and re-layouts  0.64 us (1%)
    pallas_call x1, Pallas kernels, large_call(): pl.pallas_call(functools.partial(large_kernel, members), out_shape=pltpu....  43.8 us

profile of v2, /device:TPU:0, one launch (start us, length us, event | category | flops | bytes accessed | tf_op | source)
XLA Modules:
  0.0 45.1 jit_solution(4743614428166617709)
XLA Ops:
  0.7 43.8 %shard_map.136 = bf16[64,128]{1,0:T(8,128)(2,1)S(1)} custom-call(bf16[1,8192]{1,0:T(2,128)(2,1)} %query_hbm.1, bf16[1,1024]{1,0:T(2,128)(2,1)} %key_new_hbm.1, bf16[1,1024]{1,0:T(2,128)(2,1)} %value_new_hbm.1, bf16[128,1024]{1,0:T(8,128)(2,1)} %bitcast.9, bf16[128,1024]{1,0:T(8,128)(2,1)} %bitcast.10, s32[1]{0:T(128)S(6)} %copy.18.lengths_hbm, ...), custom_call_target="tpu_custom_call" | custom-call | tf_op jit(solution)/shard_map/pallas_call | solution.py:712
  44.5 0.6 %copy.17 = bf16[1,1,64,128]{3,1,2,0:T(2,128)(2,1)} copy(bf16[1,1,64,128]{3,2,1,0:T(8,128)(2,1)S(1)} %bitcast.8) | data formatting | bytes 32768

commit v3 on v2

--- a/solution.py
+++ b/solution.py
@@ -18,8 +18,24 @@
 MESH = pl.DeviceIdType.MESH
 
 SLOTS = 28
-STAGES = ((0, 0), (0, 1), (1, 0), (1, 1))
-RELAYED = (True, False)
+CHUNKS = (
+    (0, 0, 0),
+    (0, 0, 1),
+    (0, 0, 2),
+    (0, 0, 3),
+    (0, 1, 0),
+    (0, 1, 1),
+    (0, 1, 2),
+    (0, 1, 3),
+    (1, 0, 0),
+    (1, 0, 1),
+    (1, 0, 2),
+    (1, 0, 3),
+    (1, 1, 0),
+    (1, 1, 1),
+    (1, 1, 2),
+    (1, 1, 3),
+)
 SPREAD = (0, 2, 6, 4, 1, 3, 7, 5)
 
 def large_kernel(
@@ -43,12 +59,10 @@
     route_ids,
     route_scores,
     query,
-    key_new,
-    value_new,
+    fresh_kv,
     stream,
     gain,
-    key_cache,
-    value_cache,
+    cache,
     in_sem,
     heads,
     own_rows,
@@ -90,6 +104,7 @@
     a_send,
     a_relay,
     a_recv,
+    a_mate,
     s_send,
     s_recv,
     q_send,
@@ -144,6 +159,13 @@
     def mate(d):
         return lax.rem(h + d, hsplit)
 
+    def far(i):
+        d = members - i
+        return model(d // hsplit) * hsplit + lax.rem(h + lax.rem(d, hsplit), hsplit)
+
+    def settle(ref, sem):
+        pltpu.make_async_copy(ref, ref, sem).wait()
+
     def remote(src, dst, send, recv, device):
         return pltpu.make_async_remote_copy(
             src_ref=src,
@@ -155,25 +177,20 @@
         )
 
     barrier = pltpu.get_barrier_semaphore()
-    inputs = [
-        pltpu.make_async_copy(src, dst, in_sem.at[k])
-        for k, (src, dst) in enumerate(
-            (
-                (query_hbm, query),
-                (key_hbm, key_cache),
-                (value_hbm, value_cache),
-                (key_new_hbm, key_new),
-                (value_new_hbm, value_new),
-                (lengths_hbm, lengths),
-                (ids_hbm, route_ids),
-                (scores_hbm, route_scores),
-                (stream_hbm, stream),
-                (gain_hbm.at[me], gain),
-            )
-        )
-    ]
-    for copy in inputs:
-        copy.start()
+    key_cache, value_cache = cache.at[0], cache.at[1]
+    sources = (
+        ((query_hbm, query),),
+        ((key_hbm, key_cache), (value_hbm, value_cache)),
+        ((key_new_hbm, fresh_kv.at[0]), (value_new_hbm, fresh_kv.at[1])),
+        ((lengths_hbm, lengths),),
+        ((ids_hbm, route_ids),),
+        ((scores_hbm, route_scores),),
+        ((stream_hbm, stream),),
+        ((gain_hbm.at[me], gain),),
+    )
+    for k, pairs in enumerate(sources):
+        for src, dst in pairs:
+            pltpu.make_async_copy(src, dst, in_sem.at[k]).start()
 
     @pl.loop(1, members)
     def _(d):
@@ -183,74 +200,63 @@
         return pltpu.make_async_copy(
             out_weight.at[pl.ds(k * block, block), :],
             pool.at[k // side, :, pl.ds(k % side * cols, cols)],
-            wo_sem.at[k],
-        )
-
-    def gu_slot(p, z, i, r):
-        return lax.rem(half + MSPLIT * STAGES.index((p, z)) + 2 * i + r, SLOTS)
-
-    def gu_copy(p, z, i, q):
-        r, w = q // 2, (gate_weight, up_weight)[q % 2]
+            wo_sem.at[0],
+        )
+
+    def gu_slot(c):
+        return (half + 2 * c) % SLOTS
+
+    def gu_start(c):
+        p, z, i = CHUNKS[c]
         at = pl.multiple_of(model(2 * (half - 1 - i) + 1 - z) * chunk + first[p], 128)
-        return pltpu.make_async_copy(
-            w.at[r, :, pl.ds(at, wide[p])],
-            pool.at[gu_slot(p, z, i, r), :, pl.ds(q % 2 * wide[p], wide[p])],
-            gu_sem.at[p, z * half + i, q],
-        )
-
-    def gu_start(s, i):
         for q in range(4):
-            gu_copy(*STAGES[s], i, q).start()
-
-    def down_order(k):
-        if isinstance(k, int):
-            return SPREAD[k]
-        d = 0
-        for j, to in enumerate(SPREAD):
-            d = d + jnp.where(k == j, to, 0)
-        return d
+            r, w = q // 2, (gate_weight, up_weight)[q % 2]
+            pltpu.make_async_copy(
+                w.at[r, :, pl.ds(at, wide[p])],
+                pool.at[gu_slot(c) + r, :, pl.ds(q % 2 * wide[p], wide[p])],
+                gu_sem.at[c],
+            ).start()
+
+    def arrived(c):
+        p = CHUNKS[c][0]
+        settle(pool.at[pl.ds(gu_slot(c), 2), :, pl.ds(0, 2 * wide[p])], gu_sem.at[c])
 
     def down_slot(p, k):
-        return lax.rem(half + (4 + p) * MSPLIT + k, SLOTS)
-
-    def down_copy(p, k, r):
-        at = pl.multiple_of(model(down_order(k)) * chunk + first[p], 16)
-        return pltpu.make_async_copy(
-            down_weight.at[r, pl.ds(at, wide[p]), :],
-            pool.at[down_slot(p, k), pl.ds(r * wide[p], wide[p]), :],
-            down_sem.at[p, k, r],
-        )
-
-    def down_start(p, k):
-        for j in range(2):
-            for r in range(RESIDENT):
-                down_copy(p, k + j, r).start()
-
-    def refill(p, z, i):
-        s = STAGES.index((p, z))
-        cases = (
-            (lambda: gu_start(3, i + 2), lambda: down_start(0, 2 * i - 4)),
-            (lambda: down_start(0, 2 * i + 4), lambda: down_start(1, 2 * i - 4)),
-            (lambda: down_start(1, 2 * i + 4),),
-            (),
-        )
-        for test, load in zip((i < 2, i >= 2), cases[s]):
-            pl.when(test)(load)
+        return (half + (4 + p) * MSPLIT + k) % SLOTS
+
+    def down_start(t):
+        p, k = t // MSPLIT, t % MSPLIT
+        at = pl.multiple_of(model(SPREAD[k]) * chunk + first[p], 16)
+        for r in range(RESIDENT):
+            pltpu.make_async_copy(
+                down_weight.at[r, pl.ds(at, wide[p]), :],
+                pool.at[down_slot(p, k), pl.ds(r * wide[p], wide[p]), :],
+                down_sem.at[t],
+            ).start()
+
+    def refill(c):
+        if c < 2:
+            gu_start(2 * MSPLIT - 2 + c)
+        elif c < MSPLIT + 2:
+            down_start(2 * c - 4)
+            down_start(2 * c - 3)
 
     for k in range(pieces):
         wo_copy(k).start()
 
     scale = HS ** (-0.5)
-    inputs[0].wait()
+    settle(query, in_sem.at[0])
     for n in range(NH):
         heads[n : n + 1, :] = query[:, n * HS : (n + 1) * HS].astype(f32)
 
-    for copy in inputs[1:]:
-        copy.wait()
+    for k, ref in enumerate(
+        (cache, fresh_kv, lengths, route_ids, route_scores, stream, gain), start=1
+    ):
+        settle(ref, in_sem.at[k])
 
     for g in range(KVH):
-        own_rows[0, g : g + 1, :] = key_new[:, g * HS : (g + 1) * HS].astype(f32)
-        own_rows[1, g : g + 1, :] = value_new[:, g * HS : (g + 1) * HS].astype(f32)
+        own_rows[0, g : g + 1, :] = fresh_kv[0, :, g * HS : (g + 1) * HS].astype(f32)
+        own_rows[1, g : g + 1, :] = fresh_kv[1, :, g * HS : (g + 1) * HS].astype(f32)
     wide_q = heads[...]
     s = jnp.concatenate(
         [
@@ -307,18 +313,18 @@
 
     def attn_copy(d, slot):
         return remote(
-            attn_send, attn_recv.at[slot], a_send.at[d], a_recv.at[slot], model(d) * hsplit + h
+            attn_send, attn_recv.at[slot], a_send.at[0], a_recv.at[d], model(d) * hsplit + h
         )
 
     def attn_relay(d, t, slot):
         src = attn_send if isinstance(d, int) else attn_recv.at[slot]
         return remote(
-            src, attn_recv.at[slot], a_relay.at[d, t], a_recv.at[slot], m * hsplit + t
+            src, attn_recv.at[slot], a_relay.at[0], a_mate.at[0], m * hsplit + t
         )
 
     def stream_copy(to, slot):
         return remote(
-            stream_rows.at[to], stream_recv.at[slot], s_send.at[to], s_recv.at[slot], to
+            stream_rows.at[to], stream_recv.at[slot], s_send.at[0], s_recv.at[0], to
         )
 
     @pl.loop(0, MSPLIT - 1)
@@ -337,11 +343,8 @@
         at = pl.multiple_of(slot * NH, NH)
         attn_wide[pl.ds(at, NH), :] = rows.astype(f32)
 
-    for s in range(3):
-
-        @pl.loop(0, half)
-        def _(i):
-            gu_start(s, i)
+    for c in range(2 * MSPLIT - half):
+        gu_start(c)
 
     widen(me, attn_send[...])
     stream_recv[me] = stream_rows[me]
@@ -356,21 +359,19 @@
             attn_relay(i, mate(d), slot).start()
 
         widen(slot, attn_recv[slot])
+
+    settle(attn_recv.at[pl.ds(0, MSPLIT * (hsplit - 1))], a_mate.at[0])
 
     @pl.loop(0, MSPLIT)
     def _(i):
         @pl.loop(1, hsplit)
         def _(d):
             slot = model(i) * hsplit + mate(d)
-            attn_copy(i, slot).wait_recv()
             widen(slot, attn_recv[slot])
 
-    for k in range(pieces):
-        wo_copy(k).wait()
-
-    @pl.loop(1, members)
-    def _(d):
-        stream_copy(me, peer(d)).wait_recv()
+    settle(pool.at[pl.ds(0, half)], wo_sem.at[0])
+
+    settle(stream_recv.at[pl.ds(0, members - 1)], s_recv.at[0])
 
     for j in range(members):
         stream_flat[j : j + 1, :] = stream_recv[j]
@@ -385,15 +386,15 @@
             pool[k // side, :, k % side * cols : (k % side + 1) * cols],
             preferred_element_type=f32,
         )
-    gu_start(3, 0)
-    gu_start(3, 1)
+    gu_start(2 * MSPLIT - 4)
+    gu_start(2 * MSPLIT - 3)
 
     resid = stream_flat[:, :cols] + proj.astype(bf16).astype(f32)
     resid_keep[...] = resid
     y_send[...] = (resid * gain[...]).astype(bf16)
 
     def y_copy(to, slot):
-        return remote(y_send, y_recv.at[slot], r_send.at[to], r_recv.at[slot], m * hsplit + to)
+        return remote(y_send, y_recv.at[slot], r_send.at[0], r_recv.at[0], m * hsplit + to)
 
     @pl.loop(1, hsplit)
     def _(d):
@@ -405,7 +406,7 @@
     sq_send[...] = jnp.sum(jnp.where(sub_w == lane_w, squares, 0.0), axis=0, keepdims=True)
 
     def sq_copy(to, slot):
-        return remote(sq_send, sq_recv.at[slot], q_send.at[to], q_recv.at[slot], to)
+        return remote(sq_send, sq_recv.at[slot], q_send.at[0], q_recv.at[0], to)
 
     @pl.loop(1, members)
     def _(d):
@@ -427,9 +428,7 @@
         hit = at == place.astype(jnp.int32) + r * cap
         back.append(jnp.where(hit, scales[r], 0.0))
 
-    @pl.loop(1, hsplit)
-    def _(d):
-        y_copy(h, mate(d)).wait_recv()
+    settle(y_recv.at[pl.ds(0, hsplit - 1)], r_recv.at[0])
 
     y = jnp.concatenate([y_recv[j] for j in range(hsplit)], axis=1)
     bases = [q * cap // 8 * 8 for q in range(4)]
@@ -446,7 +445,7 @@
         return remote(
             px_send[p].at[i],
             px_recv[p].at[i],
-            x_send.at[p, i],
+            x_send.at[p],
             x_recv.at[p, i],
             model(1) * hsplit + h,
         )
@@ -455,16 +454,17 @@
         return remote(
             pz_send[p].at[j],
             pz_recv[p].at[j],
-            z_send.at[p, j],
-            z_recv.at[p, j],
+            z_send.at[p],
+            z_recv.at[p],
             model(2 * (half - 1 - j)) * hsplit + h,
         )
 
-    def sums(p, z, i):
+    def sums(c):
+        p = CHUNKS[c][0]
         w = wide[p]
         slabs = [[] for _ in range(acc[p].shape[1] // 8)]
         for r in range(RESIDENT):
-            where = gu_slot(p, z, i, r)
+            where = gu_slot(c) + r
             values = [
                 jnp.dot(
                     slots_in[r, q * lead : (q + 1) * lead, :],
@@ -479,45 +479,38 @@
         empty = jnp.zeros((8, w), f32)
         return jnp.concatenate([sum(slab[1:], slab[0]) if slab else empty for slab in slabs], axis=0)
 
-    def arrived(p, z, i):
-        for q in range(4):
-            gu_copy(p, z, i, q).wait()
-
-    def gu_x(p, pair):
-        @pl.loop(0, half, step=pair)
-        def _(i):
-            for j in range(pair):
-                arrived(p, 0, i + j)
-            for j in range(pair):
-                px_send[p][i + j] = sums(p, 0, i + j)[:packed].astype(bf16)
-            for j in range(pair):
-                px_copy(p, i + j).start()
-            for j in range(pair):
-                refill(p, 0, i + j)
-
-    def gu_z(p, pair):
-        @pl.loop(0, half, step=pair)
-        def _(i):
-            for j in range(pair):
-                arrived(p, 1, i + j)
-            for j in range(pair):
-                acc[p][j] = sums(p, 1, i + j)
-            for j in range(pair):
-                refill(p, 1, i + j)
-                px_copy(p, i + j).wait_recv()
-                acc[p][j, :packed, :] += px_recv[p][i + j].astype(f32)
-
-                @pl.when(i + j < half - 1)
-                def _():
-                    pz_send[p][i + j] = acc[p][j, :packed, :].astype(bf16)
-                    pz_copy(p, i + j).start()
+    def gate_up(*cs):
+        for c in cs:
+            arrived(c)
+        for c in cs:
+            p, z, i = CHUNKS[c]
+            if z:
+                acc[p][i % 2] = sums(c)
+            else:
+                px_send[p][i] = sums(c)[:packed].astype(bf16)
+                px_copy(p, i).start()
+        for c in cs:
+            refill(c)
+        for c in cs:
+            p, z, i = CHUNKS[c]
+            if z:
+                px_copy(p, i).wait_recv()
+                acc[p][i % 2, :packed, :] += px_recv[p][i].astype(f32)
+                if i < half - 1:
+                    pz_send[p][i] = acc[p][i % 2, :packed, :].astype(bf16)
+                    pz_copy(p, i).start()
+
+    def hid_group(p, d):
+        if p == 0:
+            return d // 2 if d % 2 == 0 else 0
+        return (0, 0, 0, 0, 1, 1, 2, 2)[SPREAD.index(d)]
 
     def hid_copy(p, d, slot):
         return remote(
             hid_send[p],
             hid_recv[p].at[slot],
-            h_send.at[p, d],
-            h_recv.at[p, slot],
+            h_send.at[p],
+            h_recv.at[p, hid_group(p, d)],
             model(d) * hsplit + h,
         )
 
@@ -525,19 +518,19 @@
         return remote(
             hid_recv[p].at[slot],
             hid_recv[p].at[slot],
-            h_relay.at[p, j],
-            h_recv.at[p, slot],
+            h_relay.at[0],
+            h_recv.at[p, 0],
             model(1) * hsplit + h,
         )
 
     def finish(p, last):
+        settle(pz_recv[p], z_recv.at[p])
         for j in range(half - 1):
-            pz_copy(p, j).wait_recv()
             acc[p][last, :packed, :] += pz_recv[p][j].astype(f32)
         a = acc[p][last, :hid_rows, :] * scaled
         b = acc[p][last, 2 * cap : 2 * cap + hid_rows, :] * scaled
         hid_send[p][...] = (a / (1.0 + jnp.exp(-a)) * b).astype(bf16)
-        for d in (1, *SPREAD[1:half]) if RELAYED[p] else range(MSPLIT - 1, 0, -1):
+        for d in (1, *SPREAD[1:half]) if p == 0 else range(MSPLIT - 1, 0, -1):
             hid_copy(p, d, m).start()
         hid_recv[p][m] = hid_send[p][...]
 
@@ -548,11 +541,13 @@
             hid_relay(p, k, slot).start()
 
     def down(p, ks, fresh=False):
+        groups = {}
         for k in ks:
-            if k >= half or k and not RELAYED[p]:
-                hid_copy(p, SPREAD[k], model(SPREAD[k])).wait_recv()
-            for r in range(RESIDENT):
-                down_copy(p, k, r).wait()
+            if k >= half or k and p:
+                groups.setdefault(hid_group(p, SPREAD[k]), []).append(k)
+            settle(pool.at[down_slot(p, k), pl.ds(0, 2 * wide[p]), :], down_sem.at[p * MSPLIT + k])
+        for g, members_of in groups.items():
+            settle(hid_recv[p].at[pl.ds(0, len(members_of))], h_recv.at[p, g])
         line = lax.broadcasted_iota(jnp.int32, (hid_rows, wide[p]), 0)
         value = None if fresh else total[...]
         for k in ks:
@@ -569,15 +564,18 @@
             value = term if value is None else value + term
         total[...] = value
 
-    gu_x(0, 1)
-
-    gu_z(0, 2)
-
-    gu_x(1, 2)
-
-    @pl.loop(1, members)
-    def _(d):
-        sq_copy(me, peer(d)).wait_recv()
+    gate_up(0)
+    gate_up(1)
+    gate_up(2)
+    gate_up(3)
+
+    gate_up(4, 5)
+    gate_up(6, 7)
+
+    gate_up(8, 9)
+    gate_up(10, 11)
+
+    settle(sq_recv.at[pl.ds(0, members - 1)], q_recv.at[0])
 
     power = jnp.sum(sq_recv[...], axis=0)[:, :batch] * (1.0 / width)
     inverse = lax.rsqrt(power + 1e-05)
@@ -589,13 +587,16 @@
 
     finish(0, 1)
 
-    gu_z(1, 1)
+    gate_up(12)
+    gate_up(13)
+    gate_up(14)
+    gate_up(15)
 
     relays(0)
 
     down(0, range(half), True)
 
-    finish(1, 0)
+    finish(1, 1)
 
     down(0, range(half, MSPLIT))
 
@@ -618,48 +619,27 @@
 
     def final_copy(to, slot):
         return remote(
-            final_send.at[to], final_recv.at[slot], f_send.at[to], f_recv.at[slot], to
+            final_send.at[to], final_recv.at[slot], f_send.at[0], f_recv.at[0], to
         )
 
     @pl.loop(1, members)
     def _(d):
-        final_copy(peer(d), me).start()
+        final_copy(far(d), me).start()
 
     final_recv[me] = final_send[me]
 
-    @pl.loop(1, members)
-    def _(d):
-        to = peer(d)
-        stream_copy(to, me).wait_send()
-        sq_copy(to, me).wait_send()
-
-    @pl.loop(1, hsplit)
-    def _(d):
-        y_copy(mate(d), h).wait_send()
-
-    @pl.loop(0, MSPLIT)
-    def _(i):
-        @pl.loop(1, hsplit)
-        def _(d):
-            attn_relay(i, mate(d), me).wait_send()
-
-    @pl.loop(1, MSPLIT)
-    def _(d):
-        attn_copy(d, me).wait_send()
-
+    settle(stream_recv.at[pl.ds(0, members - 1)], s_send.at[0])
+    settle(sq_recv.at[pl.ds(0, members - 1)], q_send.at[0])
+    settle(y_recv.at[pl.ds(0, hsplit - 1)], r_send.at[0])
+    settle(attn_recv.at[pl.ds(0, MSPLIT * (hsplit - 1))], a_relay.at[0])
+    settle(attn_recv.at[pl.ds(0, MSPLIT - 1)], a_send.at[0])
     for p in range(2):
-        for i in range(half):
-            px_copy(p, i).wait_send()
-        for j in range(half - 1):
-            pz_copy(p, j).wait_send()
-        for d in (1, *SPREAD[1:half]) if RELAYED[p] else range(1, MSPLIT):
-            hid_copy(p, d, m).wait_send()
-        for j in range(1, half if RELAYED[p] else 1):
-            hid_relay(p, j, m).wait_send()
-
-    @pl.loop(1, members)
-    def _(d):
-        final_copy(me, peer(d)).wait_recv()
+        settle(px_recv[p], x_send.at[p])
+        settle(pz_recv[p], z_send.at[p])
+        settle(hid_recv[p].at[pl.ds(0, MSPLIT - 1 if p else half)], h_send.at[p])
+    settle(hid_recv[0].at[pl.ds(0, half - 1)], h_relay.at[0])
+
+    settle(final_recv.at[pl.ds(0, members - 1)], f_recv.at[0])
 
     for j in range(MSPLIT):
         line = final_recv[j * hsplit].astype(f32)
@@ -667,9 +647,7 @@
             line = line + final_recv[j * hsplit + k].astype(f32)
         out[j * tiles : (j + 1) * tiles, :] = line.astype(bf16)
 
-    @pl.loop(1, members)
-    def _(d):
-        final_copy(peer(d), me).wait_send()
+    settle(final_recv.at[pl.ds(0, members - 1)], f_send.at[0])
 
 def large_call(
     stream_in,
@@ -719,13 +697,11 @@
             pltpu.SMEM(route_ids.shape, jnp.int32),
             pltpu.SMEM(route_scores.shape, f32),
             pltpu.VMEM((1, NH * HS), bf16),
-            pltpu.VMEM((1, KVH * HS), bf16),
-            pltpu.VMEM((1, KVH * HS), bf16),
+            pltpu.VMEM((2, 1, KVH * HS), bf16),
             pltpu.VMEM((1, width), bf16),
             pltpu.VMEM((1, cols), f32),
-            pltpu.VMEM((rows, KVH * HS), bf16),
-            pltpu.VMEM((rows, KVH * HS), bf16),
-            dma((10,)),
+            pltpu.VMEM((2, rows, KVH * HS), bf16),
+            dma((8,)),
             pltpu.VMEM((NH, HS), f32),
             pltpu.VMEM((2, KVH, HS), f32),
             pltpu.VMEM((members, 1, cols + HS), f32),
@@ -753,16 +729,17 @@
             pltpu.VMEM((tiles * batch, HS), f32),
             pltpu.VMEM((members, tiles, HS), bf16),
             pltpu.VMEM((members, tiles, HS), bf16),
-            dma((NH * HS // block,)),
-            dma((2, MSPLIT, 4)),
-            dma((2, MSPLIT, RESIDENT)),
+            dma((1,)),
+            dma((2 * MSPLIT,)),
+            dma((2 * MSPLIT,)),
         ]
-        + [dma((MSPLIT,)), dma((MSPLIT, hsplit))]
-        + [dma((members,))] * 5
-        + [dma((hsplit,))] * 2
-        + [dma((2, half))] * 4
-        + [dma((2, MSPLIT)), dma((2, half)), dma((2, MSPLIT))]
-        + [dma((members,))] * 2,
+        + [dma((1,))] * 2
+        + [dma((MSPLIT,))]
+        + [dma((1,))] * 7
+        + [dma((2,)), dma((2, half))]
+        + [dma((2,))] * 3
+        + [dma((1,)), dma((2, half))]
+        + [dma((1,))] * 2,
         compiler_params=pltpu.CompilerParams(
             collective_id=0, has_side_effects=True, vmem_limit_bytes=66000000
         ),

time: 45.3 us -> 42.7 us (0.943)
  Pallas kernels: 43.8 us -> 41.2 us
    pallas_call x1, Pallas kernels: 43.8 us -> 41.2 us  [large_call(): pl.pallas_call(functools.partial(large_kernel, members), out_shape=pltpu....]
where the time goes in v3:
time: 42.7 us; the launch traced here: 42.5 us
  Pallas kernels  41.2 us (96%)
  between operations  0.66 us (2%)
  local copies, waits for them, and re-layouts  0.64 us (1%)
    pallas_call x1, Pallas kernels, large_call(): pl.pallas_call(functools.partial(large_kernel, members), out_shape=pltpu....  41.2 us

profile of v3, /device:TPU:0, one launch (start us, length us, event | category | flops | bytes accessed | tf_op | source)
XLA Modules:
  0.0 42.5 jit_solution(16844049247930613796)
XLA Ops:
  0.7 41.2 %shard_map.136 = bf16[64,128]{1,0:T(8,128)(2,1)S(1)} custom-call(bf16[1,8192]{1,0:T(2,128)(2,1)} %query_hbm.1, bf16[1,1024]{1,0:T(2,128)(2,1)} %key_new_hbm.1, bf16[1,1024]{1,0:T(2,128)(2,1)} %value_new_hbm.1, bf16[128,1024]{1,0:T(8,128)(2,1)} %bitcast.9, bf16[128,1024]{1,0:T(8,128)(2,1)} %bitcast.10, s32[1]{0:T(128)S(6)} %copy.18.lengths_hbm, ...), custom_call_target="tpu_custom_call" | custom-call | tf_op jit(solution)/shard_map/pallas_call | solution.py:690
  41.9 0.6 %copy.17 = bf16[1,1,64,128]{3,1,2,0:T(2,128)(2,1)} copy(bf16[1,1,64,128]{3,2,1,0:T(8,128)(2,1)S(1)} %bitcast.8) | data formatting | bytes 32768

commit v4 on v3

--- a/solution.py
+++ b/solution.py
@@ -150,10 +150,13 @@
         return lax.rem(me + d, members)
 
     def model(d):
-        d = jnp.asarray(d, jnp.int32)
         to = 0
         for b in (1, 2, 4):
-            to = to + lax.rem(lax.div(m, b) + lax.div(d, b), 2) * b
+            if isinstance(d, int):
+                bit = lax.rem(lax.div(m, b), 2)
+                to = to + (1 - bit if d // b % 2 else bit) * b
+            else:
+                to = to + lax.rem(lax.div(m, b) + lax.div(d, b), 2) * b
         return to
 
     def mate(d):
@@ -161,7 +164,7 @@
 
     def far(i):
         d = members - i
-        return model(d // hsplit) * hsplit + lax.rem(h + lax.rem(d, hsplit), hsplit)
+        return model(d // hsplit) * hsplit + mate(d % hsplit)
 
     def settle(ref, sem):
         pltpu.make_async_copy(ref, ref, sem).wait()
@@ -530,7 +533,7 @@
         a = acc[p][last, :hid_rows, :] * scaled
         b = acc[p][last, 2 * cap : 2 * cap + hid_rows, :] * scaled
         hid_send[p][...] = (a / (1.0 + jnp.exp(-a)) * b).astype(bf16)
-        for d in (1, *SPREAD[1:half]) if p == 0 else range(MSPLIT - 1, 0, -1):
+        for d in (1, *SPREAD[1:half]) if p == 0 else (6, 4, 2, 1, 3, 7, 5):
             hid_copy(p, d, m).start()
         hid_recv[p][m] = hid_send[p][...]
 
@@ -569,8 +572,9 @@
     gate_up(2)
     gate_up(3)
 
-    gate_up(4, 5)
-    gate_up(6, 7)
+    gate_up(4)
+    gate_up(5, 6)
+    gate_up(7)
 
     gate_up(8, 9)
     gate_up(10, 11)
@@ -592,15 +596,19 @@
     gate_up(14)
     gate_up(15)
 
+    down(0, (0,), True)
+
     relays(0)
 
-    down(0, range(half), True)
+    down(0, range(1, half))
 
     finish(1, 1)
 
+    down(1, (0,))
+
     down(0, range(half, MSPLIT))
 
-    down(1, range(half))
+    down(1, range(1, half))
 
     down(1, (4, 5))
 
@@ -622,9 +630,8 @@
             final_send.at[to], final_recv.at[slot], f_send.at[0], f_recv.at[0], to
         )
 
-    @pl.loop(1, members)
-    def _(d):
-        final_copy(far(d), me).start()
+    for i in range(1, members):
+        final_copy(far(i), me).start()
 
     final_recv[me] = final_send[me]
 

time: 42.7 us -> 41.7 us (0.977)
  Pallas kernels: 41.2 us -> 40.3 us
    pallas_call x1, Pallas kernels: 41.2 us -> 40.3 us  [large_call(): pl.pallas_call(functools.partial(large_kernel, members), out_shape=pltpu....]
where the time goes in v4:
time: 41.7 us; the launch traced here: 41.6 us
  Pallas kernels  40.3 us (97%)
  between operations  0.66 us (2%)
  local copies, waits for them, and re-layouts  0.64 us (2%)
    pallas_call x1, Pallas kernels, large_call(): pl.pallas_call(functools.partial(large_kernel, members), out_shape=pltpu....  40.3 us

profile of v4, /device:TPU:0, one launch (start us, length us, event | category | flops | bytes accessed | tf_op | source)
XLA Modules:
  0.0 41.6 jit_solution(15278676950037881886)
XLA Ops:
  0.7 40.3 %shard_map.136 = bf16[64,128]{1,0:T(8,128)(2,1)S(1)} custom-call(bf16[1,8192]{1,0:T(2,128)(2,1)} %query_hbm.1, bf16[1,1024]{1,0:T(2,128)(2,1)} %key_new_hbm.1, bf16[1,1024]{1,0:T(2,128)(2,1)} %value_new_hbm.1, bf16[128,1024]{1,0:T(8,128)(2,1)} %bitcast.9, bf16[128,1024]{1,0:T(8,128)(2,1)} %bitcast.10, s32[1]{0:T(128)S(6)} %copy.18.lengths_hbm, ...), custom_call_target="tpu_custom_call" | custom-call | tf_op jit(solution)/shard_map/pallas_call | solution.py:697
  40.9 0.6 %copy.17 = bf16[1,1,64,128]{3,1,2,0:T(2,128)(2,1)} copy(bf16[1,1,64,128]{3,2,1,0:T(8,128)(2,1)S(1)} %bitcast.8) | data formatting | bytes 32768
